TPU v7x, 32 devices: a whole 2x2x4 slice. The times are simulated.
32 devices in a mesh: tm: 8 (over y, x, core), chan: 4 (over z).
Axes of the slice: x: 2, y: 2, z: 4, core: 2. Of those that a mesh axis runs over, the one named last changes fastest.
Arguments:
- samples: bfloat16 [2, 16384, 2048], P(None, ('tm', 'chan')), may hold values from -6 to 6
- taps: float32 [8, 2048], replicated, may hold values from -2.5 to 2.5
Outputs:
- spectra: bfloat16 [2, 2, 1024, 16384], P(None, None, ('tm', 'chan'))
All inputs are finite; a program needn't handle non-finite values.
Results may differ from a plain program's by a relative error of at most 0.0055.
Values may be sent and summed in bfloat16 or wider, within the bound.
No kernel may reach another device: no remote copies, remote signals or barrier semaphores. Data moves between devices by JAX's collectives and lax.ppermute only.
A program may use at most 64 MiB of HBM per device.

v0:
```python
import jax
import jax.numpy as jnp
from jax import lax
from jax.sharding import PartitionSpec as P


def from_behind(array, axis, by):
    count = lax.axis_size(axis)
    pairs = [(i, i + by) for i in range(count) if 0 <= i + by < count]
    return lax.ppermute(array, axis, pairs)


def make_table(nfft, count):
    index_k = jnp.arange(count, dtype=jnp.int32)[:, None]
    index_n = jnp.arange(nfft, dtype=jnp.int32)[None, :]
    phase = (index_k * index_n % nfft).astype(jnp.float32)
    angle = phase * (2.0 * 3.141592653589793 / nfft)
    return jnp.stack([jnp.cos(angle) / 32.0, -jnp.sin(angle) / 32.0]).astype(jnp.bfloat16)


def local(samples, taps):
    pol_count, frames_dev, nfft = samples.shape
    tap_count = taps.shape[0]
    tail = samples[:, frames_dev - (tap_count - 1) :, :]
    prior = from_behind(tail, ("tm", "chan"), 1)
    extended = jnp.concatenate([prior, samples], axis=1)
    weighted = jnp.zeros((pol_count, frames_dev, nfft), jnp.float32)
    for tap in range(tap_count):
        weighted = weighted + taps[tap][None, None, :] * extended[
            :, tap : tap + frames_dev, :
        ].astype(jnp.float32)
    weighted = weighted.astype(jnp.bfloat16)
    table = make_table(nfft, nfft // 2)
    spectrum = jnp.einsum(
        "ckn,pfn->cpkf", table, weighted, preferred_element_type=jnp.float32
    ).astype(jnp.bfloat16)
    turned = lax.all_to_all(spectrum, ("tm", "chan"), split_axis=2, concat_axis=3, tiled=True)
    return turned


def solution(mesh):
    return jax.shard_map(
        local,
        mesh=mesh,
        in_specs=(P(None, ("tm", "chan"), None), P()),
        out_specs=P(None, None, ("tm", "chan"), None),
        check_vma=False,
    )
```

profile of v0, /device:TPU:1, one launch (start us, length us, event | category | flops | bytes accessed | tf_op | source)
XLA Modules:
  0.0 170.4 jit_solution(9282074759876690828)
XLA Ops:
  0.0 0.9 slice.49
  0.9 0.0 copy-start
  0.9 0.0 copy-start.1
  0.9 4.3 %collective-permute-start = (bf16[2,7,2048]{2,1,0:T(8,128)(2,1)S(1)}, bf16[2,7,2048]{2,1,0:T(8,128)(2,1)S(1)}, u32[]{:S(2)}, u32[]{:S(2)}) collective-permute-start(bf16[2,7,2048]{2,1,0:T(8,128)(2,1)S(1)} %slice.49), channel_id=1, source_target_pairs={{0,1},{1,2},{2,3},{3,4},{4,5},{5,6},{6,7},{7,8},{8,9},{9,10},{10,1... | collective-permute-start | bytes 172040 | tf_op jit(solution)/shard_map/ppermute | solution.py:10
  5.2 34.1 %multiply_convert_fusion = (bf16[1,1024,2048]{2,1,0:T(8,128)(2,1)S(1)}, bf16[1,1024,2048]{2,1,0:T(8,128)(2,1)S(1)}) fusion(), kind=kLoop, calls=%fused_computation.16 | loop fusion | flops 39845888 | bytes 8388608 | tf_op jit(solution)/shard_map/convert.1
  39.2 0.0 copy-done
  39.3 0.0 collective-permute-done
  39.3 0.0 copy-done.1
  39.3 17.2 %convert_bitcast_fusion = bf16[2,2,1024,512]{2,3,0,1:T(8,128)(2,1)} fusion(bf16[1,1024,2048]{2,1,0:T(8,128)(2,1)S(1)} %get-tuple-element.13, bf16[1,1024,2048]{2,1,0:T(8,128)(2,1)S(1)} %get-tuple-element.14, bf16[2,512,2048]{2,1,0:T(8,128)(2,1)S(1)} %copy-done.1, f32[2048]{0:T(1024)S(1)} %bitcast.34, bf16[2,7,2048]{2,1,0:T(8,128)(2,1)S(1)} %collective-permute-done, ...), kind=kOutput, calls=%fused_computation.34 | convolution fusion | flops 8703180800 | bytes 16900096 | tf_op jit(solution)/shard_map/ckn,pfn->cpkf/dot_general | solution.py:34
  56.6 11.2 %copy.7 = bf16[2,2,1024,512]{3,0,1,2:T(2,128)(2,1)} copy(bf16[2,2,1024,512]{2,3,0,1:T(8,128)(2,1)} %convert_bitcast_fusion) | data formatting | bytes 8388608 | tf_op jit(solution)/shard_map/convert_element_type | solution.py:36
  67.7 99.3 %all_to_all.18 = bf16[2,2,1024,512]{3,0,1,2:T(2,128)(2,1)S(1)} all-to-all(bf16[2,2,1024,512]{3,0,1,2:T(2,128)(2,1)} %copy.7), channel_id=1, replica_groups=mesh['tm'=8,'chan'=4] {'tm','chan'}, dimensions={2} | all-to-all | bytes 8388608 | tf_op jit(solution)/shard_map/all_to_all | solution.py:37
  167.0 0.8 copy.8
  167.8 2.5 %copy.11 = bf16[2,2,32,4,8,512]{5,4,2,3,1,0:T(8,128)(2,1)} copy(bf16[2,2,32,4,8,512]{5,4,3,2,1,0:T(8,128)(2,1)S(1)} %bitcast.27) | data formatting | bytes 8388608 | tf_op jit(solution)/shard_map/all_to_all | solution.py:37
  (1 shorter events, 0.0 us)
Async XLA Ops:
  0.9 38.4 %copy-start = (f32[8,2048]{1,0:T(8,128)S(1)}, f32[8,2048]{1,0:T(8,128)}, u32[]{:S(2)}) copy-start(f32[8,2048]{1,0:T(8,128)} %param.3) | copy-start | bytes 196612
  0.9 38.4 %copy-start.1 = (bf16[2,512,2048]{2,1,0:T(8,128)(2,1)S(1)}, bf16[2,512,2048]{2,1,0:T(8,128)(2,1)}, u32[]{:S(2)}) copy-start(bf16[2,512,2048]{2,1,0:T(8,128)(2,1)} %param.2) | copy-start | bytes 12582916
  0.9 38.4 %collective-permute-start = (bf16[2,7,2048]{2,1,0:T(8,128)(2,1)S(1)}, bf16[2,7,2048]{2,1,0:T(8,128)(2,1)S(1)}, u32[]{:S(2)}, u32[]{:S(2)}) collective-permute-start(bf16[2,7,2048]{2,1,0:T(8,128)(2,1)S(1)} %slice.49), channel_id=1, source_target_pairs={{0,1},{1,2},{2,3},{3,4},{4,5},{5,6},{6,7},{7,8},{8,9},{9,10},{10,1... | collective-permute-start | bytes 172040 | tf_op jit(solution)/shard_map/ppermute | solution.py:10
where the time goes:
time: 171 us; the launch traced here: 170 us
  blocking collectives  99.3 us (58%)
  other arithmetic  34.1 us (20%)
  matrix products  17.2 us (10%)
  local copies, waits for them, and re-layouts  15.4 us (9%)
  starting transfers between devices  4.29 us (3%)
    all_to_all x1, blocking collectives, local(): lax.all_to_all(spectrum, ('tm', 'chan'), split_axis=2, concat_axis=3, til...  99.3 us
    another operation x1, other arithmetic  34.1 us
    dot_general x1, matrix products, local(): jnp.einsum('ckn,pfn->cpkf', table, weighted, preferred_element_type=jnp.f...  17.2 us
    convert_element_type x1, local copies, waits for them, and re-layouts, local(): spectrum = jnp.einsum('ckn,pfn->cpkf', table, weighted, preferred_element...  11.2 us
    ppermute x1, starting transfers between devices, from_behind(): return lax.ppermute(array, axis, pairs)  4.29 us
  transfers between devices with their start and end apart: 1, of which 0 were waited for; matrix products, arithmetic and copies ran while one was open for 20% of the time, Pallas kernels for 0%

commit v1 on v0

v1 whole, which is shorter than its diff:
```python
import functools

import jax
import jax.numpy as jnp
import numpy as np
from jax import lax
from jax.experimental import pallas as pl
from jax.experimental.pallas import tpu as pltpu
from jax.sharding import PartitionSpec as P


LANES = 128
ROWS = 8
CHUNK = 128
PIECES = 4
LEAD = 1
VMEM_LIMIT = 60 * 1024 * 1024


def twiddles(nfft):
    span = nfft // LANES
    high = np.arange(nfft // 2 // span)[:, None] * span * np.arange(LANES)[None, :]
    low = np.arange(span)[:, None] * np.arange(LANES)[None, :]
    step = np.arange(span)[:, None] * np.arange(span)[None, :] * LANES

    def pair(turns):
        angle = 2.0 * np.pi * (turns % nfft) / nfft
        return np.stack([np.cos(angle), np.sin(angle)]).astype(np.float32)

    step = np.broadcast_to(pair(step)[:, :, :, None] / 32.0, (2, span, span, LANES))
    return jnp.asarray(pair(high)), jnp.asarray(pair(low)), jnp.asarray(np.ascontiguousarray(step))


def fir(load, chunks, taps_ref, weighted_ref, ext_ref):
    nfft = taps_ref.shape[1]
    tap_count = taps_ref.shape[0]
    pols = weighted_ref.shape[1] // CHUNK

    def body(step, carry):
        pol = lax.rem(step, pols)
        at = pl.ds(pl.multiple_of(step // pols * LANES, LANES), LANES)
        load(step, pol, at)
        taps = taps_ref[:, at]
        rows = 64
        for chunk in range(chunks):
            for first in range(0, CHUNK, rows):
                total = None
                for tap in range(tap_count):
                    start = ROWS + chunk * CHUNK + first + tap - (tap_count - 1)
                    term = taps[tap : tap + 1, :] * ext_ref[pl.ds(start, rows), :]
                    total = term if total is None else total + term
                to = pl.ds(pl.multiple_of(pol * CHUNK + first, rows), rows)
                weighted_ref[chunk, to, at] = total.astype(jnp.bfloat16)
        return carry

    lax.fori_loop(0, pols * nfft // LANES, body, 0)


def fill_phases(high_ref, low_ref, phase_ref):
    span = low_ref.shape[1]
    for a in range(high_ref.shape[1]):
        high_c, high_s = high_ref[0, pl.ds(a, 1), :], high_ref[1, pl.ds(a, 1), :]
        low_c, low_s = low_ref[0], low_ref[1]
        phase_ref[0, pl.ds(a * span, span), :] = high_c * low_c - high_s * low_s
        phase_ref[1, pl.ds(a * span, span), :] = -(high_s * low_c) - high_c * low_s


def fill_table(group, dest_of, own, phase_ref, step_ref, table_ref):
    span = step_ref.shape[1]
    height = 2 * ROWS if own % (2 * ROWS) == 0 and span % (2 * ROWS) == 0 else ROWS
    per = table_ref.shape[0] // (2 * own)
    for slot in range(per):
        for first in range(0, own, height):
            k = pl.multiple_of(dest_of(group * per + slot) * own + first, height)
            c, s = phase_ref[0, pl.ds(k, height), :], phase_ref[1, pl.ds(k, height), :]
            r = 0 if height == span else pl.multiple_of(lax.rem(k, span), height)
            at_c = slot * 2 * own + first
            at_s = at_c + own
            for m in range(span):
                mc, ms = step_ref[0, m, pl.ds(r, height), :], step_ref[1, m, pl.ds(r, height), :]
                lanes = pl.ds(m * LANES, LANES)
                table_ref[pl.ds(at_c, height), lanes] = (c * mc + s * ms).astype(jnp.bfloat16)
                table_ref[pl.ds(at_s, height), lanes] = (s * mc - c * ms).astype(jnp.bfloat16)


def transform(store, count, dest_of, own, weighted_ref, phase_ref, step_ref, table_refs):
    per = table_refs[0].shape[0] // (2 * own)
    groups = count // per

    def one(group, now, later):
        for chunk in range(weighted_ref.shape[0]):
            part = lax.dot_general(
                now[...],
                weighted_ref[chunk],
                (((1,), (1,)), ((), ())),
                preferred_element_type=jnp.float32,
            ).astype(jnp.bfloat16)
            for slot in range(per):
                for c in range(2):
                    row = (slot * 2 + c) * own
                    store(group * per + slot, c, chunk, part[row : row + own])
            if chunk == 0:
                fill_table(jnp.minimum(group + 1, groups - 1), dest_of, own, phase_ref, step_ref, later)

    def two(index, carry):
        one(2 * index, table_refs[0], table_refs[1])
        one(2 * index + 1, table_refs[1], table_refs[0])
        return carry

    lax.fori_loop(0, groups // 2, two, 0)
    if groups % 2:
        one(groups - 1, table_refs[0], table_refs[1])


def position(axes):
    return lax.axis_index(axes[0][0]) * axes[1][1] + lax.axis_index(axes[1][0])


def within(axes, item):
    half = axes[1][1] // 2
    return item // half * axes[1][1] + item % half


def compute_kernel(axes, kind, begin, own, samples, *refs):
    refs = list(refs)
    halo = refs.pop(0) if kind == "all" else None
    brought = refs.pop(0) if kind == "near" else None
    taps, high, low, step, out = refs[:5]
    rows, weighted, ext, phase, table, table_next, sems = refs[-7:]
    pols, _, nfft = samples.shape
    count = weighted.shape[0] * CHUNK
    pieces = sems.shape[0]
    wide = nfft // pieces
    first = 0 if halo is not None else begin - ROWS
    held = begin + count - first
    copies = [
        pltpu.make_async_copy(
            samples.at[:, pl.ds(first, held), pl.ds(piece * wide, wide)],
            rows.at[:, :, pl.ds(piece * wide, wide)],
            sems.at[piece],
        )
        for piece in range(pieces)
    ]
    for copy in copies:
        copy.start()

    half = axes[1][1] // 2
    if kind == "all":
        dest_of = lambda item: item
    else:
        me = position(axes)
        dest_of = lambda item: me ^ (within(axes, item) + (half if kind == "far" else 0))

    def store(item, c, chunk, part):
        for pol in range(pols):
            block = part[:, pol * CHUNK : (pol + 1) * CHUNK]
            if kind == "near":
                out[item, 0, c, pol] = block
            else:
                out[item, c, pol, :, pl.ds(chunk * CHUNK, CHUNK)] = block

    fill_phases(high, low, phase)
    fill_table(0, dest_of, own, phase, step, table)
    steps = wide // LANES * pols

    def load(at_step, pol, at):
        for piece, copy in enumerate(copies):
            pl.when(at_step == piece * steps)(copy.wait)
        if halo is not None:
            ext[pl.ds(0, ROWS), :] = halo[pol, :, at].astype(jnp.float32)
            ext[pl.ds(ROWS, held), :] = rows[pol, :, at].astype(jnp.float32)
        else:
            ext[...] = rows[pol, :, at].astype(jnp.float32)

    fir(load, count // CHUNK, taps, weighted, ext)
    transform(store, out.shape[0], dest_of, own, weighted, phase, step, (table, table_next))
    if kind == "near":

        def hand_on(item, carry):
            out[item, 1] = brought[item]
            return carry

        lax.fori_loop(0, out.shape[0], hand_on, 0)


def place_main_kernel(frames, block, held, out, sems):
    copies = []
    for source in range(block.shape[0]):
        at = pl.ds(source * frames, block.shape[4])
        copies.append(pltpu.make_async_copy(block.at[source], out.at[:, :, :, at], sems.at[source]))
    for copy in copies:
        copy.start()
    for copy in copies:
        copy.wait()


def place_near_kernel(axes, frames, begin, *refs):
    blocks, (mine, out, sems) = refs[:-3], refs[-3:]
    half = axes[1][1] // 2
    me = position(axes)
    copies = []
    for item in range(len(blocks) + 1):
        block = mine if item == 0 else blocks[item - 1]
        for side in range(2):
            source = me ^ (within(axes, item) + side * half)
            at = pl.ds(pl.multiple_of(source * frames + begin, CHUNK), frames - begin)
            copies.append(pltpu.make_async_copy(block.at[side], out.at[:, :, :, at], sems.at[2 * item + side]))
    for copy in copies:
        copy.start()
    for copy in copies:
        copy.wait()


def local(axes, samples, taps):
    pols, frames, nfft = samples.shape
    tap_count = taps.shape[0]
    channels = nfft // 2
    both = tuple(name for name, _ in axes)
    row_count, column_count = axes[0][1], axes[1][1]
    devices = row_count * column_count
    half = column_count // 2
    own = channels // devices
    chunks = frames // CHUNK
    per = max(1, 256 // (2 * own))
    assert own % ROWS == 0 and tap_count <= ROWS and nfft % (LANES * PIECES) == 0 and frames % CHUNK == 0 and chunks > 1
    assert devices & (devices - 1) == 0 and half > 0 and row_count * half % per == 0

    high, low, step = twiddles(nfft)
    bf16 = jnp.bfloat16
    vmem = pl.BlockSpec(memory_space=pltpu.VMEM)
    anywhere = pl.BlockSpec(memory_space=pl.ANY)
    dma = pltpu.SemaphoreType.DMA
    nears = row_count * half
    begin = (chunks - LEAD) * CHUNK
    short = frames - begin

    def compute(kind, at, count, out_shape, *extra):
        held = count * CHUNK + (0 if kind == "all" else ROWS)
        dests = devices if kind == "all" else nears
        return pl.pallas_call(
            functools.partial(compute_kernel, axes, kind, at, own),
            out_shape=[jax.ShapeDtypeStruct(shape, bf16) for shape in out_shape],
            in_specs=[anywhere] + [vmem] * (4 + len(extra)),
            out_specs=[vmem] * len(out_shape),
            scratch_shapes=[
                pltpu.VMEM((pols, held, nfft), bf16),
                pltpu.VMEM((count, pols * CHUNK, nfft), bf16),
                pltpu.VMEM((count * CHUNK + ROWS, LANES), jnp.float32),
                pltpu.VMEM((2, channels, LANES), jnp.float32),
                pltpu.VMEM((per * 2 * own, nfft), bf16),
                pltpu.VMEM((per * 2 * own, nfft), bf16),
                dma((PIECES,)),
            ],
            compiler_params=pltpu.CompilerParams(vmem_limit_bytes=VMEM_LIMIT),
            cost_estimate=pl.CostEstimate(
                flops=4 * dests * own * pols * count * CHUNK * nfft,
                bytes_accessed=2 * pols * count * CHUNK * nfft * 2,
                transcendentals=0,
            ),
        )(samples, *extra, taps, high, low, step)

    def swap(part, by):
        return lax.ppermute(part, both, [(i, i ^ by) for i in range(devices)])

    out_shape = jax.ShapeDtypeStruct((2, pols, own, devices * frames), bf16)
    small = pltpu.CompilerParams(vmem_limit_bytes=1024 * 1024)

    halo = lax.ppermute(samples[:, frames - ROWS :, :], both, [(i, i + 1) for i in range(devices - 1)])
    (part,) = compute("far", begin, LEAD, [(nears, 2, pols, own, short)])
    brought = swap(part, half)
    (part,) = compute("all", 0, chunks - LEAD, [(devices, 2, pols, own, begin)], halo)
    arrived = lax.all_to_all(part, both, split_axis=0, concat_axis=0, tiled=True)
    (part,) = compute("near", begin, LEAD, [(nears, 2, 2, pols, own, short)], brought)
    blocks = [swap(part[item], item // half * column_count + item % half) for item in range(1, nears)]
    out = pl.pallas_call(
        functools.partial(place_near_kernel, axes, frames, begin),
        out_shape=out_shape,
        in_specs=[anywhere] * (nears - 1) + [vmem],
        out_specs=anywhere,
        scratch_shapes=[dma((2 * nears,))],
        compiler_params=small,
        name="place_near",
    )(*blocks, part[0])
    return pl.pallas_call(
        functools.partial(place_main_kernel, frames),
        out_shape=out_shape,
        in_specs=[anywhere] * 2,
        out_specs=anywhere,
        scratch_shapes=[dma((devices,))],
        input_output_aliases={1: 0},
        compiler_params=small,
        name="place_main",
    )(arrived, out)


def solution(mesh):
    axes = tuple((name, mesh.shape[name]) for name in ("tm", "chan"))

    def body(samples, taps):
        return local(axes, samples, taps)

    return jax.shard_map(
        body,
        mesh=mesh,
        in_specs=(P(None, ("tm", "chan"), None), P()),
        out_specs=P(None, None, ("tm", "chan"), None),
        check_vma=False,
    )
```

time: 171 us -> 164 us (0.959); the launches traced: 170 us -> 162 us
  blocking collectives: 99.3 us -> 0 us
  waiting for transfers between devices: 0.01 us -> 94.4 us
  Pallas kernels: 0 us -> 35.4 us
  other arithmetic: 34.1 us -> 0 us
  starting transfers between devices: 4.29 us -> 28.1 us
  matrix products: 17.2 us -> 0 us
  local copies, waits for them, and re-layouts: 15.4 us -> 3.6 us
    all_to_all x1 -> x0, blocking collectives: 99.3 us -> none  [local(): lax.all_to_all(spectrum, ('tm', 'chan'), split_axis=2, concat_axis=3, til...]
    ppermute x1 -> x17, waiting for transfers between devices: 0.01 us -> 94.4 us  [the longest x16 89.8 us: swap(): return lax.ppermute(part, both, [(i, i ^ by) for i in range(devices)])]
    pallas_call x0 -> x5, Pallas kernels: none -> 35.4 us  [the longest x3 32.2 us: compute(): pl.pallas_call(functools.partial(compute_kernel, axes, kind, at, own), ou...]
    another operation x1 -> x0, other arithmetic: 34.1 us -> none
    ppermute x1 -> x17, starting transfers between devices: 4.29 us -> 23.5 us  [the longest x16 19.5 us: swap(): return lax.ppermute(part, both, [(i, i ^ by) for i in range(devices)])]
    dot_general x1 -> x0, matrix products: 17.2 us -> none  [local(): jnp.einsum('ckn,pfn->cpkf', table, weighted, preferred_element_type=jnp.f...]
    convert_element_type x1 -> x0, local copies, waits for them, and re-layouts: 11.2 us -> none  [local(): spectrum = jnp.einsum('ckn,pfn->cpkf', table, weighted, preferred_element...]
    all_to_all x0 -> x1, starting transfers between devices: none -> 4.56 us  [local(): lax.all_to_all(part, both, split_axis=0, concat_axis=0, tiled=True)]
  transfers between devices with their start and end apart: 1 -> 18, of which waited for: 0 -> 7; matrix products, arithmetic and copies ran while one was open for 20% -> 1% of each run, Pallas kernels for 0% -> 10%
where the time goes in v1:
time: 164 us; the launch traced here: 162 us
  waiting for transfers between devices  94.4 us (58%)
  Pallas kernels  35.4 us (22%)
  starting transfers between devices  28.1 us (17%)
  local copies, waits for them, and re-layouts  3.6 us (2%)
    ppermute x16, waiting for transfers between devices, swap(): return lax.ppermute(part, both, [(i, i ^ by) for i in range(devices)])  89.8 us
    pallas_call x3, Pallas kernels, compute(): pl.pallas_call(functools.partial(compute_kernel, axes, kind, at, own), ou...  32.2 us
    ppermute x16, starting transfers between devices, swap(): return lax.ppermute(part, both, [(i, i ^ by) for i in range(devices)])  19.5 us
    ppermute x1, waiting for transfers between devices, local(): lax.ppermute(samples[:, frames - ROWS:, :], both, [(i, i + 1) for i in ra...  4.66 us
    all_to_all x1, starting transfers between devices, local(): lax.all_to_all(part, both, split_axis=0, concat_axis=0, tiled=True)  4.56 us
    ppermute x1, starting transfers between devices, local(): lax.ppermute(samples[:, frames - ROWS:, :], both, [(i, i + 1) for i in ra...  4.01 us
  transfers between devices with their start and end apart: 18, of which 7 were waited for; matrix products, arithmetic and copies ran while one was open for 1% of the time, Pallas kernels for 10%

profile of v1, /device:TPU:1, one launch (start us, length us, event | category | flops | bytes accessed | tf_op | source)
XLA Modules:
  0.0 161.6 jit_solution(10405011023147453400)
XLA Ops:
  0.0 0.8 slice.51
  0.8 4.0 %collective-permute-start = (bf16[2,8,2048]{2,1,0:T(8,128)(2,1)S(1)}, bf16[2,8,2048]{2,1,0:T(8,128)(2,1)S(1)}, u32[]{:S(2)}, u32[]{:S(2)}) collective-permute-start(bf16[2,8,2048]{2,1,0:T(8,128)(2,1)S(1)} %slice.51), channel_id=1, source_target_pairs={{0,1},{1,2},{2,3},{3,4},{4,5},{5,6},{6,7},{7,8},{8,9},{9,10},{10,1... | collective-permute-start | bytes 196616 | tf_op jit(solution)/shard_map/ppermute | solution.py:268
  4.9 4.7 %collective-permute-done.refs_0_ = bf16[2,8,2048]{2,1,0:T(8,128)(2,1)S(1)} collective-permute-done((bf16[2,8,2048]{2,1,0:T(8,128)(2,1)S(1)}, bf16[2,8,2048]{2,1,0:T(8,128)(2,1)S(1)}, u32[]{:S(2)}, u32[]{:S(2)}) %collective-permute-start) | collective-permute-done | bytes 65568 | tf_op jit(solution)/shard_map/ppermute | solution.py:268
  9.5 0.6 copy-done.1
  10.2 17.9 %shard_map.55 = bf16[32,2,2,32,384]{4,3,2,1,0:T(8,128)(2,1)} custom-call(bf16[2,512,2048]{2,1,0:T(8,128)(2,1)} %samples.5, bf16[2,8,2048]{2,1,0:T(8,128)(2,1)} %copy-done.1, f32[8,2048]{1,0:T(8,128)} %refs_1_.4, f32[2,64,128]{2,1,0:T(8,128)} %constant.6.clone.refs_2_.refs_1_, f32[2,16,128]{2,1,0:T(8,128)} %constant.7.clone.refs_3_.refs_2_, ...), custom_call_target="tpu_custom_call" | custom-call | flops 6442450944 | bytes 6291456 | tf_op jit(solution)/shard_map/pallas_call | solution.py:240
  28.1 4.6 %all-to-all-start = ((bf16[32,2,2,32,384]{4,3,2,1,0:T(8,128)(2,1)}), bf16[32,2,2,32,384]{4,3,2,1,0:T(8,128)(2,1)S(1)}, u32[]{:S(2)}, u32[]{:S(2)}) async-start(bf16[32,2,2,32,384]{4,3,2,1,0:T(8,128)(2,1)} %shard_map.55), calls=%async_computation | async-start | bytes 6291456 | tf_op jit(solution)/shard_map/all_to_all | solution.py:272
  32.7 6.9 %shard_map.56 = bf16[16,2,2,32,128]{4,3,2,1,0:T(8,128)(2,1)} custom-call(bf16[2,512,2048]{2,1,0:T(8,128)(2,1)} %samples.5, f32[8,2048]{1,0:T(8,128)} %refs_1_.4, f32[2,64,128]{2,1,0:T(8,128)} %constant.6.clone.refs_2_.refs_1_, f32[2,16,128]{2,1,0:T(8,128)} %constant.7.clone.refs_3_.refs_2_, f32[2,16,16,128]{3,2,1,0:T(8,128)} %constant.8.clone.refs_4_.refs_3_), custom_call_target="tpu_custom_call" | custom-call | flops 1073741824 | bytes 2097152 | tf_op jit(solution)/shard_map/pallas_call | solution.py:240
  39.6 2.3 %collective-permute-start.1 = (bf16[16,2,2,32,128]{4,3,2,1,0:T(8,128)(2,1)}, bf16[16,2,2,32,128]{4,3,2,1,0:T(8,128)(2,1)S(1)}, u32[]{:S(2)}, u32[]{:S(2)}) collective-permute-start(bf16[16,2,2,32,128]{4,3,2,1,0:T(8,128)(2,1)} %shard_map.56), channel_id=1, source_target_pairs={{0,2},{1,3},{2,0},{3,1},{4,6},{5,7},{6,4},{7,5},{8,10},{9,11},{10,... | collective-permute-start | bytes 1572872 | tf_op jit(solution)/shard_map/ppermute | solution.py:263
  41.9 85.1 %collective-permute-done.1.refs_0_ = bf16[16,2,2,32,128]{4,3,2,1,0:T(8,128)(2,1)S(1)} collective-permute-done((bf16[16,2,2,32,128]{4,3,2,1,0:T(8,128)(2,1)}, bf16[16,2,2,32,128]{4,3,2,1,0:T(8,128)(2,1)S(1)}, u32[]{:S(2)}, u32[]{:S(2)}) %collective-permute-start.1) | collective-permute-done | bytes 524320 | tf_op jit(solution)/shard_map/ppermute | solution.py:263
  127.1 0.8 copy-done
  127.9 7.3 %shard_map.57 = bf16[16,2,2,2,32,128]{5,4,3,2,1,0:T(8,128)(2,1)} custom-call(bf16[2,512,2048]{2,1,0:T(8,128)(2,1)} %samples.5, bf16[16,2,2,32,128]{4,3,2,1,0:T(8,128)(2,1)} %copy-done, f32[8,2048]{1,0:T(8,128)} %refs_1_.4, f32[2,64,128]{2,1,0:T(8,128)} %constant.6.clone.refs_2_.refs_1_, f32[2,16,128]{2,1,0:T(8,128)} %constant.7.clone.refs_3_.refs_2_, ...), custom_call_target="tpu_custom_call" | custom-call | flops 1073741824 | bytes 2097152 | tf_op jit(solution)/shard_map/pallas_call | solution.py:240
  135.2 1.3 slice_bitcast_fusion
  136.7 1.6 %collective-permute-start.15 = (bf16[2,2,2,32,128]{4,3,2,1,0:T(8,128)(2,1)S(1)}, bf16[2,2,2,32,128]{4,3,2,1,0:T(8,128)(2,1)S(1)}, u32[]{:S(2)}, u32[]{:S(2)}) collective-permute-start(bf16[2,2,2,32,128]{4,3,2,1,0:T(8,128)(2,1)S(1)} %get-tuple-element.7), channel_id=1, source_target_pairs={{0,28},{1,29},{2,30},{3,31},{4,24},{5,25},{6,26},{7,27},{8,20},{9,... | collective-permute-start | bytes 196616 | tf_op jit(solution)/shard_map/ppermute | solution.py:263
  138.3 2.6 %collective-permute-start.14 = (bf16[2,2,2,32,128]{4,3,2,1,0:T(8,128)(2,1)S(1)}, bf16[2,2,2,32,128]{4,3,2,1,0:T(8,128)(2,1)S(1)}, u32[]{:S(2)}, u32[]{:S(2)}) collective-permute-start(bf16[2,2,2,32,128]{4,3,2,1,0:T(8,128)(2,1)S(1)} %get-tuple-element.8), channel_id=1, source_target_pairs={{0,25},{1,24},{2,27},{3,26},{4,29},{5,28},{6,31},{7,30},{8,17},{9,... | collective-permute-start | bytes 196616 | tf_op jit(solution)/shard_map/ppermute | solution.py:263
  140.9 1.6 %collective-permute-start.13 = (bf16[2,2,2,32,128]{4,3,2,1,0:T(8,128)(2,1)S(1)}, bf16[2,2,2,32,128]{4,3,2,1,0:T(8,128)(2,1)S(1)}, u32[]{:S(2)}, u32[]{:S(2)}) collective-permute-start(bf16[2,2,2,32,128]{4,3,2,1,0:T(8,128)(2,1)S(1)} %get-tuple-element.9), channel_id=1, source_target_pairs={{0,24},{1,25},{2,26},{3,27},{4,28},{5,29},{6,30},{7,31},{8,16},{9,... | collective-permute-start | bytes 196616 | tf_op jit(solution)/shard_map/ppermute | solution.py:263
  142.6 0.1 collective-permute-start.12
  142.7 0.2 collective-permute-done.16.refs_14_
  142.9 2.3 %collective-permute-start.11 = (bf16[2,2,2,32,128]{4,3,2,1,0:T(8,128)(2,1)S(1)}, bf16[2,2,2,32,128]{4,3,2,1,0:T(8,128)(2,1)S(1)}, u32[]{:S(2)}, u32[]{:S(2)}) collective-permute-start(bf16[2,2,2,32,128]{4,3,2,1,0:T(8,128)(2,1)S(1)} %get-tuple-element.11), channel_id=1, source_target_pairs={{0,20},{1,21},{2,22},{3,23},{4,16},{5,17},{6,18},{7,19},{8,28},{9,... | collective-permute-start | bytes 196616 | tf_op jit(solution)/shard_map/ppermute | solution.py:263
  145.2 1.2 collective-permute-start.10
  146.4 1.2 collective-permute-start.9
  147.6 1.5 collective-permute-start.8
  149.1 0.6 collective-permute-start.7
  149.7 1.4 collective-permute-done.11.refs_9_
  151.1 1.0 collective-permute-start.6
  152.2 0.9 collective-permute-start.5
  153.1 2.2 %collective-permute-start.4 = (bf16[2,2,2,32,128]{4,3,2,1,0:T(8,128)(2,1)S(1)}, bf16[2,2,2,32,128]{4,3,2,1,0:T(8,128)(2,1)S(1)}, u32[]{:S(2)}, u32[]{:S(2)}) collective-permute-start(bf16[2,2,2,32,128]{4,3,2,1,0:T(8,128)(2,1)S(1)} %get-tuple-element.18), channel_id=1, source_target_pairs={{0,5},{1,4},{2,7},{3,6},{4,1},{5,0},{6,3},{7,2},{8,13},{9,12},{10,... | collective-permute-start | bytes 196616 | tf_op jit(solution)/shard_map/ppermute | solution.py:263
  155.2 0.2 collective-permute-start.2
  155.4 1.6 collective-permute-done.5.refs_3_
  157.0 0.5 collective-permute-done.4.refs_2_
  157.5 0.9 collective-permute-done.2.refs_0_
  158.4 1.2 place_near.1.held
  159.7 1.9 %place_main.1 = bf16[2,2,32,16384]{3,2,1,0:T(8,128)(2,1)} custom-call(bf16[32,2,2,32,384]{4,3,2,1,0:T(8,128)(2,1)S(1)} %all-to-all-done.block, bf16[2,2,32,16384]{3,2,1,0:T(8,128)(2,1)} %place_near.1.held), custom_call_target="tpu_custom_call", output_to_operand_aliasing={{}: (1, {})} | custom-call | tf_op jit(solution)/shard_map/place_main/pallas_call | solution.py:284
  (15 shorter events, 0.1 us)
Async XLA Ops:
  0.8 8.7 %collective-permute-start = (bf16[2,8,2048]{2,1,0:T(8,128)(2,1)S(1)}, bf16[2,8,2048]{2,1,0:T(8,128)(2,1)S(1)}, u32[]{:S(2)}, u32[]{:S(2)}) collective-permute-start(bf16[2,8,2048]{2,1,0:T(8,128)(2,1)S(1)} %slice.51), channel_id=1, source_target_pairs={{0,1},{1,2},{2,3},{3,4},{4,5},{5,6},{6,7},{7,8},{8,9},{9,10},{10,1... | collective-permute-start | bytes 196616 | tf_op jit(solution)/shard_map/ppermute | solution.py:268
  9.5 0.6 copy-start.1
  28.1 131.6 %all-to-all-start = ((bf16[32,2,2,32,384]{4,3,2,1,0:T(8,128)(2,1)}), bf16[32,2,2,32,384]{4,3,2,1,0:T(8,128)(2,1)S(1)}, u32[]{:S(2)}, u32[]{:S(2)}) async-start(bf16[32,2,2,32,384]{4,3,2,1,0:T(8,128)(2,1)} %shard_map.55), calls=%async_computation | async-start | bytes 6291456 | tf_op jit(solution)/shard_map/all_to_all | solution.py:272
  39.6 87.5 %collective-permute-start.1 = (bf16[16,2,2,32,128]{4,3,2,1,0:T(8,128)(2,1)}, bf16[16,2,2,32,128]{4,3,2,1,0:T(8,128)(2,1)S(1)}, u32[]{:S(2)}, u32[]{:S(2)}) collective-permute-start(bf16[16,2,2,32,128]{4,3,2,1,0:T(8,128)(2,1)} %shard_map.56), channel_id=1, source_target_pairs={{0,2},{1,3},{2,0},{3,1},{4,6},{5,7},{6,4},{7,5},{8,10},{9,11},{10,... | collective-permute-start | bytes 1572872 | tf_op jit(solution)/shard_map/ppermute | solution.py:263
  127.1 0.8 copy-start
  136.6 6.3 %collective-permute-start.16 = (bf16[2,2,2,32,128]{4,3,2,1,0:T(8,128)(2,1)S(1)}, bf16[2,2,2,32,128]{4,3,2,1,0:T(8,128)(2,1)S(1)}, u32[]{:S(2)}, u32[]{:S(2)}) collective-permute-start(bf16[2,2,2,32,128]{4,3,2,1,0:T(8,128)(2,1)S(1)} %get-tuple-element.6), channel_id=1, source_target_pairs={{0,29},{1,28},{2,31},{3,30},{4,25},{5,24},{6,27},{7,26},{8,21},{9,... | collective-permute-start | bytes 196616 | tf_op jit(solution)/shard_map/ppermute | solution.py:263
  136.7 8.5 %collective-permute-start.15 = (bf16[2,2,2,32,128]{4,3,2,1,0:T(8,128)(2,1)S(1)}, bf16[2,2,2,32,128]{4,3,2,1,0:T(8,128)(2,1)S(1)}, u32[]{:S(2)}, u32[]{:S(2)}) collective-permute-start(bf16[2,2,2,32,128]{4,3,2,1,0:T(8,128)(2,1)S(1)} %get-tuple-element.7), channel_id=1, source_target_pairs={{0,28},{1,29},{2,30},{3,31},{4,24},{5,25},{6,26},{7,27},{8,20},{9,... | collective-permute-start | bytes 196616 | tf_op jit(solution)/shard_map/ppermute | solution.py:263
  138.3 8.1 %collective-permute-start.14 = (bf16[2,2,2,32,128]{4,3,2,1,0:T(8,128)(2,1)S(1)}, bf16[2,2,2,32,128]{4,3,2,1,0:T(8,128)(2,1)S(1)}, u32[]{:S(2)}, u32[]{:S(2)}) collective-permute-start(bf16[2,2,2,32,128]{4,3,2,1,0:T(8,128)(2,1)S(1)} %get-tuple-element.8), channel_id=1, source_target_pairs={{0,25},{1,24},{2,27},{3,26},{4,29},{5,28},{6,31},{7,30},{8,17},{9,... | collective-permute-start | bytes 196616 | tf_op jit(solution)/shard_map/ppermute | solution.py:263
  140.9 6.7 %collective-permute-start.13 = (bf16[2,2,2,32,128]{4,3,2,1,0:T(8,128)(2,1)S(1)}, bf16[2,2,2,32,128]{4,3,2,1,0:T(8,128)(2,1)S(1)}, u32[]{:S(2)}, u32[]{:S(2)}) collective-permute-start(bf16[2,2,2,32,128]{4,3,2,1,0:T(8,128)(2,1)S(1)} %get-tuple-element.9), channel_id=1, source_target_pairs={{0,24},{1,25},{2,26},{3,27},{4,28},{5,29},{6,30},{7,31},{8,16},{9,... | collective-permute-start | bytes 196616 | tf_op jit(solution)/shard_map/ppermute | solution.py:263
  142.6 6.6 %collective-permute-start.12 = (bf16[2,2,2,32,128]{4,3,2,1,0:T(8,128)(2,1)S(1)}, bf16[2,2,2,32,128]{4,3,2,1,0:T(8,128)(2,1)S(1)}, u32[]{:S(2)}, u32[]{:S(2)}) collective-permute-start(bf16[2,2,2,32,128]{4,3,2,1,0:T(8,128)(2,1)S(1)} %get-tuple-element.10), channel_id=1, source_target_pairs={{0,21},{1,20},{2,23},{3,22},{4,17},{5,16},{6,19},{7,18},{8,29},{9,... | collective-permute-start | bytes 196616 | tf_op jit(solution)/shard_map/ppermute | solution.py:263
  142.9 8.3 %collective-permute-start.11 = (bf16[2,2,2,32,128]{4,3,2,1,0:T(8,128)(2,1)S(1)}, bf16[2,2,2,32,128]{4,3,2,1,0:T(8,128)(2,1)S(1)}, u32[]{:S(2)}, u32[]{:S(2)}) collective-permute-start(bf16[2,2,2,32,128]{4,3,2,1,0:T(8,128)(2,1)S(1)} %get-tuple-element.11), channel_id=1, source_target_pairs={{0,20},{1,21},{2,22},{3,23},{4,16},{5,17},{6,18},{7,19},{8,28},{9,... | collective-permute-start | bytes 196616 | tf_op jit(solution)/shard_map/ppermute | solution.py:263
  145.2 7.0 %collective-permute-start.10 = (bf16[2,2,2,32,128]{4,3,2,1,0:T(8,128)(2,1)S(1)}, bf16[2,2,2,32,128]{4,3,2,1,0:T(8,128)(2,1)S(1)}, u32[]{:S(2)}, u32[]{:S(2)}) collective-permute-start(bf16[2,2,2,32,128]{4,3,2,1,0:T(8,128)(2,1)S(1)} %get-tuple-element.12), channel_id=1, source_target_pairs={{0,17},{1,16},{2,19},{3,18},{4,21},{5,20},{6,23},{7,22},{8,25},{9,... | collective-permute-start | bytes 196616 | tf_op jit(solution)/shard_map/ppermute | solution.py:263
  146.4 6.6 %collective-permute-start.9 = (bf16[2,2,2,32,128]{4,3,2,1,0:T(8,128)(2,1)S(1)}, bf16[2,2,2,32,128]{4,3,2,1,0:T(8,128)(2,1)S(1)}, u32[]{:S(2)}, u32[]{:S(2)}) collective-permute-start(bf16[2,2,2,32,128]{4,3,2,1,0:T(8,128)(2,1)S(1)} %get-tuple-element.13), channel_id=1, source_target_pairs={{0,16},{1,17},{2,18},{3,19},{4,20},{5,21},{6,22},{7,23},{8,24},{9,... | collective-permute-start | bytes 196616 | tf_op jit(solution)/shard_map/ppermute | solution.py:263
  147.6 7.6 %collective-permute-start.8 = (bf16[2,2,2,32,128]{4,3,2,1,0:T(8,128)(2,1)S(1)}, bf16[2,2,2,32,128]{4,3,2,1,0:T(8,128)(2,1)S(1)}, u32[]{:S(2)}, u32[]{:S(2)}) collective-permute-start(bf16[2,2,2,32,128]{4,3,2,1,0:T(8,128)(2,1)S(1)} %get-tuple-element.14), channel_id=1, source_target_pairs={{0,13},{1,12},{2,15},{3,14},{4,9},{5,8},{6,11},{7,10},{8,5},{9,4},... | collective-permute-start | bytes 196616 | tf_op jit(solution)/shard_map/ppermute | solution.py:263
  149.1 6.1 %collective-permute-start.7 = (bf16[2,2,2,32,128]{4,3,2,1,0:T(8,128)(2,1)S(1)}, bf16[2,2,2,32,128]{4,3,2,1,0:T(8,128)(2,1)S(1)}, u32[]{:S(2)}, u32[]{:S(2)}) collective-permute-start(bf16[2,2,2,32,128]{4,3,2,1,0:T(8,128)(2,1)S(1)} %get-tuple-element.15), channel_id=1, source_target_pairs={{0,12},{1,13},{2,14},{3,15},{4,8},{5,9},{6,10},{7,11},{8,4},{9,5},... | collective-permute-start | bytes 196616 | tf_op jit(solution)/shard_map/ppermute | solution.py:263
  151.1 4.3 %collective-permute-start.6 = (bf16[2,2,2,32,128]{4,3,2,1,0:T(8,128)(2,1)S(1)}, bf16[2,2,2,32,128]{4,3,2,1,0:T(8,128)(2,1)S(1)}, u32[]{:S(2)}, u32[]{:S(2)}) collective-permute-start(bf16[2,2,2,32,128]{4,3,2,1,0:T(8,128)(2,1)S(1)} %get-tuple-element.16), channel_id=1, source_target_pairs={{0,9},{1,8},{2,11},{3,10},{4,13},{5,12},{6,15},{7,14},{8,1},{9,0},... | collective-permute-start | bytes 196616 | tf_op jit(solution)/shard_map/ppermute | solution.py:263
  152.2 4.9 %collective-permute-start.5 = (bf16[2,2,2,32,128]{4,3,2,1,0:T(8,128)(2,1)S(1)}, bf16[2,2,2,32,128]{4,3,2,1,0:T(8,128)(2,1)S(1)}, u32[]{:S(2)}, u32[]{:S(2)}) collective-permute-start(bf16[2,2,2,32,128]{4,3,2,1,0:T(8,128)(2,1)S(1)} %get-tuple-element.17), channel_id=1, source_target_pairs={{0,8},{1,9},{2,10},{3,11},{4,12},{5,13},{6,14},{7,15},{8,0},{9,1},... | collective-permute-start | bytes 196616 | tf_op jit(solution)/shard_map/ppermute | solution.py:263
  153.1 4.4 %collective-permute-start.4 = (bf16[2,2,2,32,128]{4,3,2,1,0:T(8,128)(2,1)S(1)}, bf16[2,2,2,32,128]{4,3,2,1,0:T(8,128)(2,1)S(1)}, u32[]{:S(2)}, u32[]{:S(2)}) collective-permute-start(bf16[2,2,2,32,128]{4,3,2,1,0:T(8,128)(2,1)S(1)} %get-tuple-element.18), channel_id=1, source_target_pairs={{0,5},{1,4},{2,7},{3,6},{4,1},{5,0},{6,3},{7,2},{8,13},{9,12},{10,... | collective-permute-start | bytes 196616 | tf_op jit(solution)/shard_map/ppermute | solution.py:263
  155.2 2.2 %collective-permute-start.3 = (bf16[2,2,2,32,128]{4,3,2,1,0:T(8,128)(2,1)S(1)}, bf16[2,2,2,32,128]{4,3,2,1,0:T(8,128)(2,1)S(1)}, u32[]{:S(2)}, u32[]{:S(2)}) collective-permute-start(bf16[2,2,2,32,128]{4,3,2,1,0:T(8,128)(2,1)S(1)} %get-tuple-element.19), channel_id=1, source_target_pairs={{0,4},{1,5},{2,6},{3,7},{4,0},{5,1},{6,2},{7,3},{8,12},{9,13},{10,... | collective-permute-start | bytes 196616 | tf_op jit(solution)/shard_map/ppermute | solution.py:263
  155.2 3.2 %collective-permute-start.2 = (bf16[2,2,2,32,128]{4,3,2,1,0:T(8,128)(2,1)S(1)}, bf16[2,2,2,32,128]{4,3,2,1,0:T(8,128)(2,1)S(1)}, u32[]{:S(2)}, u32[]{:S(2)}) collective-permute-start(bf16[2,2,2,32,128]{4,3,2,1,0:T(8,128)(2,1)S(1)} %get-tuple-element.20), channel_id=1, source_target_pairs={{0,1},{1,0},{2,3},{3,2},{4,5},{5,4},{6,7},{7,6},{8,9},{9,8},{10,11... | collective-permute-start | bytes 196616 | tf_op jit(solution)/shard_map/ppermute | solution.py:263

commit v2 on v1

v2 whole, which is shorter than its diff:
```python
import functools

import jax
import jax.numpy as jnp
import numpy as np
from jax import lax
from jax.experimental import pallas as pl
from jax.experimental.pallas import tpu as pltpu
from jax.sharding import PartitionSpec as P


LANES = 128
ROWS = 8
CHUNK = 128
PIECES = 4
LEAD = 1
VMEM_LIMIT = 60 * 1024 * 1024


def twiddles(nfft, radix):
    span = nfft // LANES
    r = np.arange(span).reshape(-1, radix).T.reshape(-1)
    high = np.arange(nfft // 2 // span)[:, None] * span * np.arange(LANES)[None, :]
    low = r[:, None] * np.arange(LANES)[None, :]
    step = np.arange(span // radix)[:, None] * r[None, :] * LANES

    def pair(turns):
        angle = 2.0 * np.pi * (turns % nfft) / nfft
        return np.stack([np.cos(angle), np.sin(angle)]).astype(np.float32)

    step = np.broadcast_to(pair(step)[:, :, :, None] / 32.0, (2, span // radix, span, LANES))
    return jnp.asarray(pair(high)), jnp.asarray(pair(low)), jnp.asarray(np.ascontiguousarray(step))


def fir(load, chunks, taps_ref, weighted_ref, ext_ref):
    nfft = taps_ref.shape[1]
    tap_count = taps_ref.shape[0]
    radix = weighted_ref.shape[0]
    pols = weighted_ref.shape[2] // CHUNK
    width = nfft // radix
    rows = 64 // radix

    def body(step, carry):
        pol = lax.rem(step, pols)
        lane = pl.multiple_of(step // pols * LANES, LANES)
        taps = []
        for part in range(radix):
            at = pl.ds(lane + part * width, LANES)
            load(step, pol, part, at)
            taps.append(taps_ref[:, at])
        for chunk in range(chunks):
            for first in range(0, CHUNK, rows):
                totals = []
                for part in range(radix):
                    total = None
                    for tap in range(tap_count):
                        start = ROWS + chunk * CHUNK + first + tap - (tap_count - 1)
                        term = taps[part][tap : tap + 1, :] * ext_ref[part, pl.ds(start, rows), :]
                        total = term if total is None else total + term
                    totals.append(total)
                to = pl.ds(pl.multiple_of(pol * CHUNK + first, rows), rows)
                if radix == 2:
                    totals = [totals[0] + totals[1], totals[0] - totals[1]]
                for part in range(radix):
                    weighted_ref[part, chunk, to, pl.ds(lane, LANES)] = totals[part].astype(jnp.bfloat16)
        return carry

    lax.fori_loop(0, pols * width // LANES, body, 0)


def fill_phases(high_ref, low_ref, phase_ref):
    span = low_ref.shape[1]
    for a in range(high_ref.shape[1]):
        high_c, high_s = high_ref[0, pl.ds(a, 1), :], high_ref[1, pl.ds(a, 1), :]
        low_c, low_s = low_ref[0], low_ref[1]
        phase_ref[0, pl.ds(a * span, span), :] = high_c * low_c - high_s * low_s
        phase_ref[1, pl.ds(a * span, span), :] = -(high_s * low_c) - high_c * low_s


def fill_table(group, dest_of, own, phase_ref, step_ref, table_ref):
    radix = table_ref.shape[0]
    steps, span = step_ref.shape[1:3]
    per = table_ref.shape[1] * radix // (2 * own)
    height = min(own, span) // radix
    blocks = own * radix // (height * radix * radix)
    for slot in range(per):
        k = dest_of(group * per + slot) * own
        for part in range(radix):
            at = part * (span // radix)
            inner = 0 if height * radix == span else pl.multiple_of(lax.rem(k, span), ROWS)
            base = pl.multiple_of(k - inner, span)
            joined = lambda pieces: pieces[0] if len(pieces) == 1 else jnp.concatenate(pieces)
            rows = [pl.ds(pl.multiple_of(base + block * span + at + inner, ROWS), height) for block in range(blocks)]
            c = joined([phase_ref[0, r, :] for r in rows])
            s = joined([phase_ref[1, r, :] for r in rows])
            to_c = slot * 2 * own // radix
            to_s = to_c + own // radix
            for m in range(steps):
                of = pl.ds(pl.multiple_of(at + inner, ROWS), height)
                mc = joined([step_ref[0, m, of, :]] * blocks)
                ms = joined([step_ref[1, m, of, :]] * blocks)
                lanes = pl.ds(m * LANES, LANES)
                table_ref[part, pl.ds(to_c, own // radix), lanes] = (c * mc + s * ms).astype(jnp.bfloat16)
                table_ref[part, pl.ds(to_s, own // radix), lanes] = (s * mc - c * ms).astype(jnp.bfloat16)


def transform(store, send, count, dest_of, own, weighted_ref, phase_ref, step_ref, table_refs, mixed_ref):
    radix, rows, _ = table_refs[0].shape
    per = rows * radix // (2 * own)
    groups = count // per

    def one(group, now, later):
        for chunk in range(weighted_ref.shape[1]):
            for part in range(radix):
                found = lax.dot_general(
                    now[part],
                    weighted_ref[part, chunk],
                    (((1,), (1,)), ((), ())),
                    preferred_element_type=jnp.float32,
                )
                for side in range(mixed_ref.shape[0]):
                    to = pl.ds(part, rows, stride=radix) if radix > 1 else pl.ds(0, rows)
                    mixed_ref[side, to, :] = found[:, side * LANES : (side + 1) * LANES]
            for slot in range(per):
                for c in range(2):
                    row = pl.ds((slot * 2 + c) * own, own)
                    store(group * per + slot, c, chunk, [mixed_ref[side, row, :] for side in range(mixed_ref.shape[0])])
            if chunk == 0:
                fill_table(jnp.minimum(group + 1, groups - 1), dest_of, own, phase_ref, step_ref, later)

    def two(index, carry):
        one(2 * index, table_refs[0], table_refs[1])
        one(2 * index + 1, table_refs[1], table_refs[0])
        send(index).start()
        return carry

    lax.fori_loop(0, groups // 2, two, 0)

    def settle(index, carry):
        send(index).wait()
        return carry

    lax.fori_loop(0, groups // 2, settle, 0)


def position(axes):
    return lax.axis_index(axes[0][0]) * axes[1][1] + lax.axis_index(axes[1][0])


def within(axes, item):
    half = axes[1][1] // 2
    return item // half * axes[1][1] + item % half


def compute_kernel(axes, kind, begin, own, samples, *refs):
    refs = list(refs)
    halo = refs.pop(0) if kind == "all" else None
    brought = refs.pop(0) if kind == "near" else None
    result = refs[4]
    rows, weighted, ext, phase, table, table_next, mixed, out, taps, high, low, step, sems, constant_sems, out_sems = refs[5:]
    pols, _, nfft = samples.shape
    radix = weighted.shape[0]
    count = weighted.shape[1] * CHUNK
    pieces = sems.shape[0]
    width = nfft // radix
    wide = width // pieces
    first = 0 if halo is not None else begin - ROWS
    held = begin + count - first
    copies = [
        pltpu.make_async_copy(
            samples.at[:, pl.ds(first, held), pl.ds(part * width + piece * wide, wide)],
            rows.at[:, :, pl.ds(part * width + piece * wide, wide)],
            sems.at[piece, part],
        )
        for piece in range(pieces)
        for part in range(radix)
    ]
    constants = [
        pltpu.make_async_copy(source, to, constant_sems.at[i])
        for i, (source, to) in enumerate(zip(refs[:4], (taps, high, low, step)))
    ]
    for copy in copies + constants:
        copy.start()

    half = axes[1][1] // 2
    if kind == "all":
        dest_of = lambda item: item
    else:
        me = position(axes)
        dest_of = lambda item: me ^ (within(axes, item) + (half if kind == "far" else 0))

    together = result.shape[0] // out_sems.shape[0]

    def send(index):
        items = pl.ds(index * together, together)
        return pltpu.make_async_copy(out.at[items], result.at[items], out_sems.at[index])

    def store(item, c, chunk, part):
        for pol in range(pols):
            block = part[pol].astype(jnp.bfloat16)
            if kind == "near":
                out[item, 0, c, pol] = block
                out[item, 1, c, pol] = brought[item, c, pol]
            else:
                out[item, c, pol, :, pl.ds(chunk * CHUNK, CHUNK)] = block

    for copy in constants:
        copy.wait()
    fill_phases(high, low, phase)
    fill_table(0, dest_of, own, phase, step, table)
    steps = wide // LANES * pols

    def load(at_step, pol, part, at):
        for piece in range(pieces):
            pl.when(at_step == piece * steps)(copies[piece * radix + part].wait)
        if halo is not None:
            ext[part, pl.ds(0, ROWS), :] = halo[pol, :, at].astype(jnp.float32)
            ext[part, pl.ds(ROWS, held), :] = rows[pol, :, at].astype(jnp.float32)
        else:
            ext[part] = rows[pol, :, at].astype(jnp.float32)

    fir(load, count // CHUNK, taps, weighted, ext)
    transform(store, send, out.shape[0], dest_of, own, weighted, phase, step, (table, table_next), mixed)


def place_main_kernel(frames, block, held, out, sems):
    copies = []
    for source in range(block.shape[0]):
        at = pl.ds(source * frames, block.shape[4])
        copies.append(pltpu.make_async_copy(block.at[source], out.at[:, :, :, at], sems.at[source]))
    for copy in copies:
        copy.start()
    for copy in copies:
        copy.wait()


def place_near_kernel(axes, frames, begin, *refs):
    blocks, (mine, out, sems) = refs[:-3], refs[-3:]
    half = axes[1][1] // 2
    me = position(axes)
    copies = []
    for item in range(len(blocks) + 1):
        block = mine if item == 0 else blocks[item - 1]
        for side in range(2):
            source = me ^ (within(axes, item) + side * half)
            at = pl.ds(pl.multiple_of(source * frames + begin, CHUNK), frames - begin)
            copies.append(pltpu.make_async_copy(block.at[side], out.at[:, :, :, at], sems.at[2 * item + side]))
    for copy in copies:
        copy.start()
    for copy in copies:
        copy.wait()


def local(axes, samples, taps):
    pols, frames, nfft = samples.shape
    tap_count = taps.shape[0]
    channels = nfft // 2
    both = tuple(name for name, _ in axes)
    row_count, column_count = axes[0][1], axes[1][1]
    devices = row_count * column_count
    half = column_count // 2
    own = channels // devices
    chunks = frames // CHUNK
    radix = 2 if own % (nfft // LANES) == 0 else 1
    per = max(1, 256 * radix // (2 * own))
    assert own % ROWS == 0 and tap_count <= ROWS and nfft % (LANES * PIECES * radix) == 0 and frames % CHUNK == 0 and chunks > 1
    assert devices & (devices - 1) == 0 and half > 0 and row_count * half % (2 * per) == 0

    high, low, step = twiddles(nfft, radix)
    bf16 = jnp.bfloat16
    vmem = pl.BlockSpec(memory_space=pltpu.VMEM)
    anywhere = pl.BlockSpec(memory_space=pl.ANY)
    hbm = pl.BlockSpec(memory_space=pltpu.HBM)
    dma = pltpu.SemaphoreType.DMA
    nears = row_count * half
    begin = (chunks - LEAD) * CHUNK
    short = frames - begin

    def compute(kind, at, count, shape, *extra):
        held = count * CHUNK + (0 if kind == "all" else ROWS)
        dests = devices if kind == "all" else nears
        return pl.pallas_call(
            functools.partial(compute_kernel, axes, kind, at, own),
            out_shape=jax.ShapeDtypeStruct(shape, bf16),
            in_specs=[hbm] + [vmem] * len(extra) + [hbm] * 4,
            out_specs=hbm,
            scratch_shapes=[
                pltpu.VMEM((pols, held, nfft), bf16),
                pltpu.VMEM((radix, count, pols * CHUNK, nfft // radix), bf16),
                pltpu.VMEM((radix, count * CHUNK + ROWS, LANES), jnp.float32),
                pltpu.VMEM((2, channels, LANES), jnp.float32),
                pltpu.VMEM((radix, per * 2 * own // radix, nfft // radix), bf16),
                pltpu.VMEM((radix, per * 2 * own // radix, nfft // radix), bf16),
                pltpu.VMEM((pols * CHUNK // LANES, per * 2 * own, LANES), jnp.float32),
                pltpu.VMEM(shape, bf16),
                pltpu.VMEM(taps.shape, taps.dtype),
                *(pltpu.VMEM(factor.shape, factor.dtype) for factor in (high, low, step)),
                dma((PIECES, radix)),
                dma((4,)),
                dma((dests // (2 * per),)),
            ],
            compiler_params=pltpu.CompilerParams(vmem_limit_bytes=VMEM_LIMIT),
            cost_estimate=pl.CostEstimate(
                flops=4 * dests * own * pols * count * CHUNK * nfft,
                bytes_accessed=2 * pols * count * CHUNK * nfft * 2,
                transcendentals=0,
            ),
        )(samples, *extra, taps, high, low, step)

    def swap(part, by):
        return lax.ppermute(part, both, [(i, i ^ by) for i in range(devices)])

    out_shape = jax.ShapeDtypeStruct((2, pols, own, devices * frames), bf16)
    small = pltpu.CompilerParams(vmem_limit_bytes=1024 * 1024)

    halo = lax.ppermute(samples[:, frames - ROWS :, :], both, [(i, i + 1) for i in range(devices - 1)])
    part = compute("far", begin, LEAD, (nears, 2, pols, own, short))
    brought = swap(part, half)
    part = compute("all", 0, chunks - LEAD, (devices, 2, pols, own, begin), halo)
    arrived = lax.all_to_all(part, both, split_axis=0, concat_axis=0, tiled=True)
    part = compute("near", begin, LEAD, (nears, 2, 2, pols, own, short), brought)
    blocks = [swap(part[item], item // half * column_count + item % half) for item in range(1, nears)]
    out = pl.pallas_call(
        functools.partial(place_near_kernel, axes, frames, begin),
        out_shape=out_shape,
        in_specs=[anywhere] * (nears - 1) + [vmem],
        out_specs=anywhere,
        scratch_shapes=[dma((2 * nears,))],
        compiler_params=small,
        name="place_near",
    )(*blocks, part[0])
    return pl.pallas_call(
        functools.partial(place_main_kernel, frames),
        out_shape=out_shape,
        in_specs=[anywhere] * 2,
        out_specs=anywhere,
        scratch_shapes=[dma((devices,))],
        input_output_aliases={1: 0},
        compiler_params=small,
        name="place_main",
    )(arrived, out)


def solution(mesh):
    axes = tuple((name, mesh.shape[name]) for name in ("tm", "chan"))

    def body(samples, taps):
        return local(axes, samples, taps)

    return jax.shard_map(
        body,
        mesh=mesh,
        in_specs=(P(None, ("tm", "chan"), None), P()),
        out_specs=P(None, None, ("tm", "chan"), None),
        check_vma=False,
    )
```

time: 164 us -> 159 us (0.970)
  Pallas kernels: 35.4 us -> 29.9 us
    pallas_call x3, Pallas kernels: 32.2 us -> 26.8 us  [compute(): pl.pallas_call(functools.partial(compute_kernel, axes, kind, at, own), ou...]
  transfers between devices with their start and end apart: 18 -> 18, of which waited for: 7 -> 7; matrix products, arithmetic and copies ran while one was open for 1% -> 1% of each run, Pallas kernels for 10% -> 9%
where the time goes in v2:
time: 159 us; the launch traced here: 157 us
  waiting for transfers between devices  95.7 us (60%)
  Pallas kernels  29.9 us (19%)
  starting transfers between devices  28.1 us (18%)
  local copies, waits for them, and re-layouts  3.6 us (2%)
    ppermute x16, waiting for transfers between devices, swap(): return lax.ppermute(part, both, [(i, i ^ by) for i in range(devices)])  91 us
    pallas_call x3, Pallas kernels, compute(): pl.pallas_call(functools.partial(compute_kernel, axes, kind, at, own), ou...  26.8 us
    ppermute x16, starting transfers between devices, swap(): return lax.ppermute(part, both, [(i, i ^ by) for i in range(devices)])  19.5 us
    ppermute x1, waiting for transfers between devices, local(): lax.ppermute(samples[:, frames - ROWS:, :], both, [(i, i + 1) for i in ra...  4.66 us
    all_to_all x1, starting transfers between devices, local(): lax.all_to_all(part, both, split_axis=0, concat_axis=0, tiled=True)  4.56 us
    ppermute x1, starting transfers between devices, local(): lax.ppermute(samples[:, frames - ROWS:, :], both, [(i, i + 1) for i in ra...  4.01 us
  transfers between devices with their start and end apart: 18, of which 7 were waited for; matrix products, arithmetic and copies ran while one was open for 1% of the time, Pallas kernels for 9%

profile of v2, /device:TPU:1, one launch (start us, length us, event | category | flops | bytes accessed | tf_op | source)
XLA Modules:
  0.0 157.3 jit_solution(10056584838427605742)
XLA Ops:
  0.0 0.8 slice.51
  0.8 4.0 %collective-permute-start = (bf16[2,8,2048]{2,1,0:T(8,128)(2,1)S(1)}, bf16[2,8,2048]{2,1,0:T(8,128)(2,1)S(1)}, u32[]{:S(2)}, u32[]{:S(2)}) collective-permute-start(bf16[2,8,2048]{2,1,0:T(8,128)(2,1)S(1)} %slice.51), channel_id=1, source_target_pairs={{0,1},{1,2},{2,3},{3,4},{4,5},{5,6},{6,7},{7,8},{8,9},{9,10},{10,1... | collective-permute-start | bytes 196616 | tf_op jit(solution)/shard_map/ppermute | solution.py:316
  4.9 4.7 %collective-permute-done.refs_0_ = bf16[2,8,2048]{2,1,0:T(8,128)(2,1)S(1)} collective-permute-done((bf16[2,8,2048]{2,1,0:T(8,128)(2,1)S(1)}, bf16[2,8,2048]{2,1,0:T(8,128)(2,1)S(1)}, u32[]{:S(2)}, u32[]{:S(2)}) %collective-permute-start) | collective-permute-done | bytes 65568 | tf_op jit(solution)/shard_map/ppermute | solution.py:316
  9.5 0.6 copy-done.1
  10.2 14.1 %shard_map.55 = bf16[32,2,2,32,384]{4,3,2,1,0:T(8,128)(2,1)} custom-call(bf16[2,512,2048]{2,1,0:T(8,128)(2,1)} %samples.5, bf16[2,8,2048]{2,1,0:T(8,128)(2,1)} %copy-done.1, f32[8,2048]{1,0:T(8,128)} %refs_1_.4, f32[2,64,128]{2,1,0:T(8,128)} %constant.6.clone.refs_2_.refs_1_, f32[2,16,128]{2,1,0:T(8,128)} %constant.7.clone.refs_3_.refs_2_, ...), custom_call_target="tpu_custom_call" | custom-call | flops 6442450944 | bytes 6291456 | tf_op jit(solution)/shard_map/pallas_call | solution.py:282
  24.3 4.6 %all-to-all-start = ((bf16[32,2,2,32,384]{4,3,2,1,0:T(8,128)(2,1)}), bf16[32,2,2,32,384]{4,3,2,1,0:T(8,128)(2,1)S(1)}, u32[]{:S(2)}, u32[]{:S(2)}) async-start(bf16[32,2,2,32,384]{4,3,2,1,0:T(8,128)(2,1)} %shard_map.55), calls=%async_computation | async-start | bytes 6291456 | tf_op jit(solution)/shard_map/all_to_all | solution.py:320
  28.8 5.7 %shard_map.56 = bf16[16,2,2,32,128]{4,3,2,1,0:T(8,128)(2,1)} custom-call(bf16[2,512,2048]{2,1,0:T(8,128)(2,1)} %samples.5, f32[8,2048]{1,0:T(8,128)} %refs_1_.4, f32[2,64,128]{2,1,0:T(8,128)} %constant.6.clone.refs_2_.refs_1_, f32[2,16,128]{2,1,0:T(8,128)} %constant.7.clone.refs_3_.refs_2_, f32[2,8,16,128]{3,2,1,0:T(8,128)} %constant.8.clone.refs_4_.refs_3_), custom_call_target="tpu_custom_call" | custom-call | flops 1073741824 | bytes 2097152 | tf_op jit(solution)/shard_map/pallas_call | solution.py:282
  34.6 2.3 %collective-permute-start.1 = (bf16[16,2,2,32,128]{4,3,2,1,0:T(8,128)(2,1)}, bf16[16,2,2,32,128]{4,3,2,1,0:T(8,128)(2,1)S(1)}, u32[]{:S(2)}, u32[]{:S(2)}) collective-permute-start(bf16[16,2,2,32,128]{4,3,2,1,0:T(8,128)(2,1)} %shard_map.56), channel_id=1, source_target_pairs={{0,2},{1,3},{2,0},{3,1},{4,6},{5,7},{6,4},{7,5},{8,10},{9,11},{10,... | collective-permute-start | bytes 1572872 | tf_op jit(solution)/shard_map/ppermute | solution.py:311
  36.9 86.3 %collective-permute-done.1.refs_0_ = bf16[16,2,2,32,128]{4,3,2,1,0:T(8,128)(2,1)S(1)} collective-permute-done((bf16[16,2,2,32,128]{4,3,2,1,0:T(8,128)(2,1)}, bf16[16,2,2,32,128]{4,3,2,1,0:T(8,128)(2,1)S(1)}, u32[]{:S(2)}, u32[]{:S(2)}) %collective-permute-start.1) | collective-permute-done | bytes 524320 | tf_op jit(solution)/shard_map/ppermute | solution.py:311
  123.2 0.8 copy-done
  124.0 6.9 %shard_map.57 = bf16[16,2,2,2,32,128]{5,4,3,2,1,0:T(8,128)(2,1)} custom-call(bf16[2,512,2048]{2,1,0:T(8,128)(2,1)} %samples.5, bf16[16,2,2,32,128]{4,3,2,1,0:T(8,128)(2,1)} %copy-done, f32[8,2048]{1,0:T(8,128)} %refs_1_.4, f32[2,64,128]{2,1,0:T(8,128)} %constant.6.clone.refs_2_.refs_1_, f32[2,16,128]{2,1,0:T(8,128)} %constant.7.clone.refs_3_.refs_2_, ...), custom_call_target="tpu_custom_call" | custom-call | flops 1073741824 | bytes 2097152 | tf_op jit(solution)/shard_map/pallas_call | solution.py:282
  131.0 1.3 slice_bitcast_fusion
  132.4 1.7 %collective-permute-start.15 = (bf16[2,2,2,32,128]{4,3,2,1,0:T(8,128)(2,1)S(1)}, bf16[2,2,2,32,128]{4,3,2,1,0:T(8,128)(2,1)S(1)}, u32[]{:S(2)}, u32[]{:S(2)}) collective-permute-start(bf16[2,2,2,32,128]{4,3,2,1,0:T(8,128)(2,1)S(1)} %get-tuple-element.7), channel_id=1, source_target_pairs={{0,28},{1,29},{2,30},{3,31},{4,24},{5,25},{6,26},{7,27},{8,20},{9,... | collective-permute-start | bytes 196616 | tf_op jit(solution)/shard_map/ppermute | solution.py:311
  134.1 2.6 %collective-permute-start.14 = (bf16[2,2,2,32,128]{4,3,2,1,0:T(8,128)(2,1)S(1)}, bf16[2,2,2,32,128]{4,3,2,1,0:T(8,128)(2,1)S(1)}, u32[]{:S(2)}, u32[]{:S(2)}) collective-permute-start(bf16[2,2,2,32,128]{4,3,2,1,0:T(8,128)(2,1)S(1)} %get-tuple-element.8), channel_id=1, source_target_pairs={{0,25},{1,24},{2,27},{3,26},{4,29},{5,28},{6,31},{7,30},{8,17},{9,... | collective-permute-start | bytes 196616 | tf_op jit(solution)/shard_map/ppermute | solution.py:311
  136.7 1.6 %collective-permute-start.13 = (bf16[2,2,2,32,128]{4,3,2,1,0:T(8,128)(2,1)S(1)}, bf16[2,2,2,32,128]{4,3,2,1,0:T(8,128)(2,1)S(1)}, u32[]{:S(2)}, u32[]{:S(2)}) collective-permute-start(bf16[2,2,2,32,128]{4,3,2,1,0:T(8,128)(2,1)S(1)} %get-tuple-element.9), channel_id=1, source_target_pairs={{0,24},{1,25},{2,26},{3,27},{4,28},{5,29},{6,30},{7,31},{8,16},{9,... | collective-permute-start | bytes 196616 | tf_op jit(solution)/shard_map/ppermute | solution.py:311
  138.3 0.1 collective-permute-start.12
  138.4 0.2 collective-permute-done.16.refs_14_
  138.6 2.3 %collective-permute-start.11 = (bf16[2,2,2,32,128]{4,3,2,1,0:T(8,128)(2,1)S(1)}, bf16[2,2,2,32,128]{4,3,2,1,0:T(8,128)(2,1)S(1)}, u32[]{:S(2)}, u32[]{:S(2)}) collective-permute-start(bf16[2,2,2,32,128]{4,3,2,1,0:T(8,128)(2,1)S(1)} %get-tuple-element.11), channel_id=1, source_target_pairs={{0,20},{1,21},{2,22},{3,23},{4,16},{5,17},{6,18},{7,19},{8,28},{9,... | collective-permute-start | bytes 196616 | tf_op jit(solution)/shard_map/ppermute | solution.py:311
  140.9 1.2 collective-permute-start.10
  142.2 1.2 collective-permute-start.9
  143.4 1.5 collective-permute-start.8
  144.9 0.6 collective-permute-start.7
  145.5 1.4 collective-permute-done.11.refs_9_
  146.9 1.0 collective-permute-start.6
  147.9 0.9 collective-permute-start.5
  148.8 2.2 %collective-permute-start.4 = (bf16[2,2,2,32,128]{4,3,2,1,0:T(8,128)(2,1)S(1)}, bf16[2,2,2,32,128]{4,3,2,1,0:T(8,128)(2,1)S(1)}, u32[]{:S(2)}, u32[]{:S(2)}) collective-permute-start(bf16[2,2,2,32,128]{4,3,2,1,0:T(8,128)(2,1)S(1)} %get-tuple-element.18), channel_id=1, source_target_pairs={{0,5},{1,4},{2,7},{3,6},{4,1},{5,0},{6,3},{7,2},{8,13},{9,12},{10,... | collective-permute-start | bytes 196616 | tf_op jit(solution)/shard_map/ppermute | solution.py:311
  151.0 0.2 collective-permute-start.2
  151.2 1.6 %collective-permute-done.5.refs_3_ = bf16[2,2,2,32,128]{4,3,2,1,0:T(8,128)(2,1)S(1)} collective-permute-done((bf16[2,2,2,32,128]{4,3,2,1,0:T(8,128)(2,1)S(1)}, bf16[2,2,2,32,128]{4,3,2,1,0:T(8,128)(2,1)S(1)}, u32[]{:S(2)}, u32[]{:S(2)}) %collective-permute-start.5) | collective-permute-done | bytes 65568 | tf_op jit(solution)/shard_map/ppermute | solution.py:311
  152.8 0.5 collective-permute-done.4.refs_2_
  153.2 0.9 collective-permute-done.2.refs_0_
  154.2 1.2 place_near.1.held
  155.4 1.9 %place_main.1 = bf16[2,2,32,16384]{3,2,1,0:T(8,128)(2,1)} custom-call(bf16[32,2,2,32,384]{4,3,2,1,0:T(8,128)(2,1)S(1)} %all-to-all-done.block, bf16[2,2,32,16384]{3,2,1,0:T(8,128)(2,1)} %place_near.1.held), custom_call_target="tpu_custom_call", output_to_operand_aliasing={{}: (1, {})} | custom-call | tf_op jit(solution)/shard_map/place_main/pallas_call | solution.py:332
  (15 shorter events, 0.1 us)
Async XLA Ops:
  0.8 8.7 %collective-permute-start = (bf16[2,8,2048]{2,1,0:T(8,128)(2,1)S(1)}, bf16[2,8,2048]{2,1,0:T(8,128)(2,1)S(1)}, u32[]{:S(2)}, u32[]{:S(2)}) collective-permute-start(bf16[2,8,2048]{2,1,0:T(8,128)(2,1)S(1)} %slice.51), channel_id=1, source_target_pairs={{0,1},{1,2},{2,3},{3,4},{4,5},{5,6},{6,7},{7,8},{8,9},{9,10},{10,1... | collective-permute-start | bytes 196616 | tf_op jit(solution)/shard_map/ppermute | solution.py:316
  9.5 0.6 copy-start.1
  24.3 131.2 %all-to-all-start = ((bf16[32,2,2,32,384]{4,3,2,1,0:T(8,128)(2,1)}), bf16[32,2,2,32,384]{4,3,2,1,0:T(8,128)(2,1)S(1)}, u32[]{:S(2)}, u32[]{:S(2)}) async-start(bf16[32,2,2,32,384]{4,3,2,1,0:T(8,128)(2,1)} %shard_map.55), calls=%async_computation | async-start | bytes 6291456 | tf_op jit(solution)/shard_map/all_to_all | solution.py:320
  34.6 88.7 %collective-permute-start.1 = (bf16[16,2,2,32,128]{4,3,2,1,0:T(8,128)(2,1)}, bf16[16,2,2,32,128]{4,3,2,1,0:T(8,128)(2,1)S(1)}, u32[]{:S(2)}, u32[]{:S(2)}) collective-permute-start(bf16[16,2,2,32,128]{4,3,2,1,0:T(8,128)(2,1)} %shard_map.56), channel_id=1, source_target_pairs={{0,2},{1,3},{2,0},{3,1},{4,6},{5,7},{6,4},{7,5},{8,10},{9,11},{10,... | collective-permute-start | bytes 1572872 | tf_op jit(solution)/shard_map/ppermute | solution.py:311
  123.2 0.8 copy-start
  132.3 6.3 %collective-permute-start.16 = (bf16[2,2,2,32,128]{4,3,2,1,0:T(8,128)(2,1)S(1)}, bf16[2,2,2,32,128]{4,3,2,1,0:T(8,128)(2,1)S(1)}, u32[]{:S(2)}, u32[]{:S(2)}) collective-permute-start(bf16[2,2,2,32,128]{4,3,2,1,0:T(8,128)(2,1)S(1)} %get-tuple-element.6), channel_id=1, source_target_pairs={{0,29},{1,28},{2,31},{3,30},{4,25},{5,24},{6,27},{7,26},{8,21},{9,... | collective-permute-start | bytes 196616 | tf_op jit(solution)/shard_map/ppermute | solution.py:311
  132.4 8.5 %collective-permute-start.15 = (bf16[2,2,2,32,128]{4,3,2,1,0:T(8,128)(2,1)S(1)}, bf16[2,2,2,32,128]{4,3,2,1,0:T(8,128)(2,1)S(1)}, u32[]{:S(2)}, u32[]{:S(2)}) collective-permute-start(bf16[2,2,2,32,128]{4,3,2,1,0:T(8,128)(2,1)S(1)} %get-tuple-element.7), channel_id=1, source_target_pairs={{0,28},{1,29},{2,30},{3,31},{4,24},{5,25},{6,26},{7,27},{8,20},{9,... | collective-permute-start | bytes 196616 | tf_op jit(solution)/shard_map/ppermute | solution.py:311
  134.1 8.1 %collective-permute-start.14 = (bf16[2,2,2,32,128]{4,3,2,1,0:T(8,128)(2,1)S(1)}, bf16[2,2,2,32,128]{4,3,2,1,0:T(8,128)(2,1)S(1)}, u32[]{:S(2)}, u32[]{:S(2)}) collective-permute-start(bf16[2,2,2,32,128]{4,3,2,1,0:T(8,128)(2,1)S(1)} %get-tuple-element.8), channel_id=1, source_target_pairs={{0,25},{1,24},{2,27},{3,26},{4,29},{5,28},{6,31},{7,30},{8,17},{9,... | collective-permute-start | bytes 196616 | tf_op jit(solution)/shard_map/ppermute | solution.py:311
  136.7 6.7 %collective-permute-start.13 = (bf16[2,2,2,32,128]{4,3,2,1,0:T(8,128)(2,1)S(1)}, bf16[2,2,2,32,128]{4,3,2,1,0:T(8,128)(2,1)S(1)}, u32[]{:S(2)}, u32[]{:S(2)}) collective-permute-start(bf16[2,2,2,32,128]{4,3,2,1,0:T(8,128)(2,1)S(1)} %get-tuple-element.9), channel_id=1, source_target_pairs={{0,24},{1,25},{2,26},{3,27},{4,28},{5,29},{6,30},{7,31},{8,16},{9,... | collective-permute-start | bytes 196616 | tf_op jit(solution)/shard_map/ppermute | solution.py:311
  138.3 6.6 %collective-permute-start.12 = (bf16[2,2,2,32,128]{4,3,2,1,0:T(8,128)(2,1)S(1)}, bf16[2,2,2,32,128]{4,3,2,1,0:T(8,128)(2,1)S(1)}, u32[]{:S(2)}, u32[]{:S(2)}) collective-permute-start(bf16[2,2,2,32,128]{4,3,2,1,0:T(8,128)(2,1)S(1)} %get-tuple-element.10), channel_id=1, source_target_pairs={{0,21},{1,20},{2,23},{3,22},{4,17},{5,16},{6,19},{7,18},{8,29},{9,... | collective-permute-start | bytes 196616 | tf_op jit(solution)/shard_map/ppermute | solution.py:311
  138.6 8.3 %collective-permute-start.11 = (bf16[2,2,2,32,128]{4,3,2,1,0:T(8,128)(2,1)S(1)}, bf16[2,2,2,32,128]{4,3,2,1,0:T(8,128)(2,1)S(1)}, u32[]{:S(2)}, u32[]{:S(2)}) collective-permute-start(bf16[2,2,2,32,128]{4,3,2,1,0:T(8,128)(2,1)S(1)} %get-tuple-element.11), channel_id=1, source_target_pairs={{0,20},{1,21},{2,22},{3,23},{4,16},{5,17},{6,18},{7,19},{8,28},{9,... | collective-permute-start | bytes 196616 | tf_op jit(solution)/shard_map/ppermute | solution.py:311
  140.9 7.0 %collective-permute-start.10 = (bf16[2,2,2,32,128]{4,3,2,1,0:T(8,128)(2,1)S(1)}, bf16[2,2,2,32,128]{4,3,2,1,0:T(8,128)(2,1)S(1)}, u32[]{:S(2)}, u32[]{:S(2)}) collective-permute-start(bf16[2,2,2,32,128]{4,3,2,1,0:T(8,128)(2,1)S(1)} %get-tuple-element.12), channel_id=1, source_target_pairs={{0,17},{1,16},{2,19},{3,18},{4,21},{5,20},{6,23},{7,22},{8,25},{9,... | collective-permute-start | bytes 196616 | tf_op jit(solution)/shard_map/ppermute | solution.py:311
  142.2 6.7 %collective-permute-start.9 = (bf16[2,2,2,32,128]{4,3,2,1,0:T(8,128)(2,1)S(1)}, bf16[2,2,2,32,128]{4,3,2,1,0:T(8,128)(2,1)S(1)}, u32[]{:S(2)}, u32[]{:S(2)}) collective-permute-start(bf16[2,2,2,32,128]{4,3,2,1,0:T(8,128)(2,1)S(1)} %get-tuple-element.13), channel_id=1, source_target_pairs={{0,16},{1,17},{2,18},{3,19},{4,20},{5,21},{6,22},{7,23},{8,24},{9,... | collective-permute-start | bytes 196616 | tf_op jit(solution)/shard_map/ppermute | solution.py:311
  143.4 7.6 %collective-permute-start.8 = (bf16[2,2,2,32,128]{4,3,2,1,0:T(8,128)(2,1)S(1)}, bf16[2,2,2,32,128]{4,3,2,1,0:T(8,128)(2,1)S(1)}, u32[]{:S(2)}, u32[]{:S(2)}) collective-permute-start(bf16[2,2,2,32,128]{4,3,2,1,0:T(8,128)(2,1)S(1)} %get-tuple-element.14), channel_id=1, source_target_pairs={{0,13},{1,12},{2,15},{3,14},{4,9},{5,8},{6,11},{7,10},{8,5},{9,4},... | collective-permute-start | bytes 196616 | tf_op jit(solution)/shard_map/ppermute | solution.py:311
  144.9 6.1 %collective-permute-start.7 = (bf16[2,2,2,32,128]{4,3,2,1,0:T(8,128)(2,1)S(1)}, bf16[2,2,2,32,128]{4,3,2,1,0:T(8,128)(2,1)S(1)}, u32[]{:S(2)}, u32[]{:S(2)}) collective-permute-start(bf16[2,2,2,32,128]{4,3,2,1,0:T(8,128)(2,1)S(1)} %get-tuple-element.15), channel_id=1, source_target_pairs={{0,12},{1,13},{2,14},{3,15},{4,8},{5,9},{6,10},{7,11},{8,4},{9,5},... | collective-permute-start | bytes 196616 | tf_op jit(solution)/shard_map/ppermute | solution.py:311
  146.9 4.3 %collective-permute-start.6 = (bf16[2,2,2,32,128]{4,3,2,1,0:T(8,128)(2,1)S(1)}, bf16[2,2,2,32,128]{4,3,2,1,0:T(8,128)(2,1)S(1)}, u32[]{:S(2)}, u32[]{:S(2)}) collective-permute-start(bf16[2,2,2,32,128]{4,3,2,1,0:T(8,128)(2,1)S(1)} %get-tuple-element.16), channel_id=1, source_target_pairs={{0,9},{1,8},{2,11},{3,10},{4,13},{5,12},{6,15},{7,14},{8,1},{9,0},... | collective-permute-start | bytes 196616 | tf_op jit(solution)/shard_map/ppermute | solution.py:311
  147.9 4.9 %collective-permute-start.5 = (bf16[2,2,2,32,128]{4,3,2,1,0:T(8,128)(2,1)S(1)}, bf16[2,2,2,32,128]{4,3,2,1,0:T(8,128)(2,1)S(1)}, u32[]{:S(2)}, u32[]{:S(2)}) collective-permute-start(bf16[2,2,2,32,128]{4,3,2,1,0:T(8,128)(2,1)S(1)} %get-tuple-element.17), channel_id=1, source_target_pairs={{0,8},{1,9},{2,10},{3,11},{4,12},{5,13},{6,14},{7,15},{8,0},{9,1},... | collective-permute-start | bytes 196616 | tf_op jit(solution)/shard_map/ppermute | solution.py:311
  148.8 4.4 %collective-permute-start.4 = (bf16[2,2,2,32,128]{4,3,2,1,0:T(8,128)(2,1)S(1)}, bf16[2,2,2,32,128]{4,3,2,1,0:T(8,128)(2,1)S(1)}, u32[]{:S(2)}, u32[]{:S(2)}) collective-permute-start(bf16[2,2,2,32,128]{4,3,2,1,0:T(8,128)(2,1)S(1)} %get-tuple-element.18), channel_id=1, source_target_pairs={{0,5},{1,4},{2,7},{3,6},{4,1},{5,0},{6,3},{7,2},{8,13},{9,12},{10,... | collective-permute-start | bytes 196616 | tf_op jit(solution)/shard_map/ppermute | solution.py:311
  151.0 2.2 %collective-permute-start.3 = (bf16[2,2,2,32,128]{4,3,2,1,0:T(8,128)(2,1)S(1)}, bf16[2,2,2,32,128]{4,3,2,1,0:T(8,128)(2,1)S(1)}, u32[]{:S(2)}, u32[]{:S(2)}) collective-permute-start(bf16[2,2,2,32,128]{4,3,2,1,0:T(8,128)(2,1)S(1)} %get-tuple-element.19), channel_id=1, source_target_pairs={{0,4},{1,5},{2,6},{3,7},{4,0},{5,1},{6,2},{7,3},{8,12},{9,13},{10,... | collective-permute-start | bytes 196616 | tf_op jit(solution)/shard_map/ppermute | solution.py:311
  151.0 3.2 %collective-permute-start.2 = (bf16[2,2,2,32,128]{4,3,2,1,0:T(8,128)(2,1)S(1)}, bf16[2,2,2,32,128]{4,3,2,1,0:T(8,128)(2,1)S(1)}, u32[]{:S(2)}, u32[]{:S(2)}) collective-permute-start(bf16[2,2,2,32,128]{4,3,2,1,0:T(8,128)(2,1)S(1)} %get-tuple-element.20), channel_id=1, source_target_pairs={{0,1},{1,0},{2,3},{3,2},{4,5},{5,4},{6,7},{7,6},{8,9},{9,8},{10,11... | collective-permute-start | bytes 196616 | tf_op jit(solution)/shard_map/ppermute | solution.py:311

commit v3 on v2

--- a/solution.py
+++ b/solution.py
@@ -14,7 +14,7 @@
 CHUNK = 128
 PIECES = 4
 LEAD = 1
-VMEM_LIMIT = 60 * 1024 * 1024
+VMEM_LIMIT = 24 * 1024 * 1024
 
 
 def twiddles(nfft, radix):
@@ -104,7 +104,7 @@
                 table_ref[part, pl.ds(to_s, own // radix), lanes] = (s * mc - c * ms).astype(jnp.bfloat16)
 
 
-def transform(store, send, count, dest_of, own, weighted_ref, phase_ref, step_ref, table_refs, mixed_ref):
+def transform(store, count, dest_of, own, weighted_ref, phase_ref, step_ref, table_refs, mixed_ref):
     radix, rows, _ = table_refs[0].shape
     per = rows * radix // (2 * own)
     groups = count // per
@@ -125,22 +125,19 @@
                 for c in range(2):
                     row = pl.ds((slot * 2 + c) * own, own)
                     store(group * per + slot, c, chunk, [mixed_ref[side, row, :] for side in range(mixed_ref.shape[0])])
-            if chunk == 0:
+            if chunk == 0 and later is not None:
                 fill_table(jnp.minimum(group + 1, groups - 1), dest_of, own, phase_ref, step_ref, later)
 
     def two(index, carry):
         one(2 * index, table_refs[0], table_refs[1])
         one(2 * index + 1, table_refs[1], table_refs[0])
-        send(index).start()
         return carry
 
-    lax.fori_loop(0, groups // 2, two, 0)
-
-    def settle(index, carry):
-        send(index).wait()
-        return carry
-
-    lax.fori_loop(0, groups // 2, settle, 0)
+    if groups == 2:
+        one(0, table_refs[0], table_refs[1])
+        one(1, table_refs[1], None)
+    else:
+        lax.fori_loop(0, groups // 2, two, 0)
 
 
 def position(axes):
@@ -150,14 +147,58 @@
 def within(axes, item):
     half = axes[1][1] // 2
     return item // half * axes[1][1] + item % half
+
+
+def prepare_kernel(axes, begin, own, samples, taps, high, low, step, *refs):
+    tail, rows, taps_out, step_out, phase, table, high_in, low_in, sems = refs
+    frames = samples.shape[1]
+    last = pl.ds(begin - ROWS, frames - begin + ROWS)
+    moves = [
+        (high, high_in),
+        (low, low_in),
+        (step, step_out),
+        (samples.at[:, pl.ds(frames - ROWS, ROWS)], tail),
+        (samples.at[:, last], rows),
+        (taps, taps_out),
+    ]
+    copies = [pltpu.make_async_copy(source, to, sems.at[i]) for i, (source, to) in enumerate(moves)]
+    for copy in copies:
+        copy.start()
+    for copy in copies[:3]:
+        copy.wait()
+    fill_phases(high_in, low_in, phase)
+    me = position(axes)
+    fill_table(0, lambda item: me ^ (within(axes, item) + axes[1][1] // 2), own, phase, step_out, table)
+    for copy in copies[3:]:
+        copy.wait()
+
+
+def far_kernel(axes, own, rows, taps, step, phase, table, out, weighted, ext, table_next, table_spare, mixed):
+    me = position(axes)
+    dest_of = lambda item: me ^ (within(axes, item) + axes[1][1] // 2)
+
+    def load(at_step, pol, part, at):
+        ext[part] = rows[pol, :, at].astype(jnp.float32)
+
+    def store(item, c, chunk, part):
+        for pol in range(out.shape[2]):
+            out[item, c, pol, :, pl.ds(chunk * CHUNK, CHUNK)] = part[pol].astype(jnp.bfloat16)
+
+    fir(load, weighted.shape[1], taps, weighted, ext)
+    radix, height, _ = table.shape
+    first = table
+    if out.shape[0] != 2 * (height * radix // (2 * own)):
+        table_spare[...] = table[...]
+        first = table_spare
+    transform(store, out.shape[0], dest_of, own, weighted, phase, step, (first, table_next), mixed)
 
 
 def compute_kernel(axes, kind, begin, own, samples, *refs):
     refs = list(refs)
     halo = refs.pop(0) if kind == "all" else None
     brought = refs.pop(0) if kind == "near" else None
-    result = refs[4]
-    rows, weighted, ext, phase, table, table_next, mixed, out, taps, high, low, step, sems, constant_sems, out_sems = refs[5:]
+    out = refs[4]
+    rows, weighted, ext, phase, table, table_next, mixed, taps, high, low, step, sems, constant_sems = refs[5:]
     pols, _, nfft = samples.shape
     radix = weighted.shape[0]
     count = weighted.shape[1] * CHUNK
@@ -179,21 +220,14 @@
         pltpu.make_async_copy(source, to, constant_sems.at[i])
         for i, (source, to) in enumerate(zip(refs[:4], (taps, high, low, step)))
     ]
-    for copy in copies + constants:
+    for copy in constants + copies:
         copy.start()
 
-    half = axes[1][1] // 2
     if kind == "all":
         dest_of = lambda item: item
     else:
         me = position(axes)
-        dest_of = lambda item: me ^ (within(axes, item) + (half if kind == "far" else 0))
-
-    together = result.shape[0] // out_sems.shape[0]
-
-    def send(index):
-        items = pl.ds(index * together, together)
-        return pltpu.make_async_copy(out.at[items], result.at[items], out_sems.at[index])
+        dest_of = lambda item: me ^ within(axes, item)
 
     def store(item, c, chunk, part):
         for pol in range(pols):
@@ -220,7 +254,7 @@
             ext[part] = rows[pol, :, at].astype(jnp.float32)
 
     fir(load, count // CHUNK, taps, weighted, ext)
-    transform(store, send, out.shape[0], dest_of, own, weighted, phase, step, (table, table_next), mixed)
+    transform(store, out.shape[0], dest_of, own, weighted, phase, step, (table, table_next), mixed)
 
 
 def place_main_kernel(frames, block, held, out, sems):
@@ -276,14 +310,16 @@
     begin = (chunks - LEAD) * CHUNK
     short = frames - begin
 
+    fixed = [pltpu.with_memory_space_constraint(x, pltpu.HBM) for x in (samples, taps, high, low, step)]
+
     def compute(kind, at, count, shape, *extra):
         held = count * CHUNK + (0 if kind == "all" else ROWS)
         dests = devices if kind == "all" else nears
         return pl.pallas_call(
             functools.partial(compute_kernel, axes, kind, at, own),
-            out_shape=jax.ShapeDtypeStruct(shape, bf16),
+            out_shape=(pltpu.HBM if kind == "all" else pltpu.VMEM)(shape, bf16),
             in_specs=[hbm] + [vmem] * len(extra) + [hbm] * 4,
-            out_specs=hbm,
+            out_specs=vmem,
             scratch_shapes=[
                 pltpu.VMEM((pols, held, nfft), bf16),
                 pltpu.VMEM((radix, count, pols * CHUNK, nfft // radix), bf16),
@@ -292,12 +328,10 @@
                 pltpu.VMEM((radix, per * 2 * own // radix, nfft // radix), bf16),
                 pltpu.VMEM((radix, per * 2 * own // radix, nfft // radix), bf16),
                 pltpu.VMEM((pols * CHUNK // LANES, per * 2 * own, LANES), jnp.float32),
-                pltpu.VMEM(shape, bf16),
                 pltpu.VMEM(taps.shape, taps.dtype),
                 *(pltpu.VMEM(factor.shape, factor.dtype) for factor in (high, low, step)),
                 dma((PIECES, radix)),
                 dma((4,)),
-                dma((dests // (2 * per),)),
             ],
             compiler_params=pltpu.CompilerParams(vmem_limit_bytes=VMEM_LIMIT),
             cost_estimate=pl.CostEstimate(
@@ -305,7 +339,7 @@
                 bytes_accessed=2 * pols * count * CHUNK * nfft * 2,
                 transcendentals=0,
             ),
-        )(samples, *extra, taps, high, low, step)
+        )(fixed[0], *extra, *fixed[1:])
 
     def swap(part, by):
         return lax.ppermute(part, both, [(i, i ^ by) for i in range(devices)])
@@ -313,8 +347,42 @@
     out_shape = jax.ShapeDtypeStruct((2, pols, own, devices * frames), bf16)
     small = pltpu.CompilerParams(vmem_limit_bytes=1024 * 1024)
 
-    halo = lax.ppermute(samples[:, frames - ROWS :, :], both, [(i, i + 1) for i in range(devices - 1)])
-    part = compute("far", begin, LEAD, (nears, 2, pols, own, short))
+    tables = (radix, per * 2 * own // radix, nfft // radix)
+    tail, *ready = pl.pallas_call(
+        functools.partial(prepare_kernel, axes, begin, own),
+        out_shape=[
+            pltpu.VMEM((pols, ROWS, nfft), bf16),
+            pltpu.VMEM((pols, short + ROWS, nfft), bf16),
+            pltpu.VMEM(taps.shape, taps.dtype),
+            pltpu.VMEM(step.shape, step.dtype),
+            pltpu.VMEM((2, channels, LANES), jnp.float32),
+            pltpu.VMEM(tables, bf16),
+        ],
+        in_specs=[hbm] * 5,
+        out_specs=[vmem] * 6,
+        scratch_shapes=[pltpu.VMEM(high.shape, high.dtype), pltpu.VMEM(low.shape, low.dtype), dma((6,))],
+        compiler_params=pltpu.CompilerParams(vmem_limit_bytes=VMEM_LIMIT),
+        name="prepare",
+    )(*fixed)
+    halo = lax.ppermute(tail, both, [(i, i + 1) for i in range(devices - 1)])
+    part = pl.pallas_call(
+        functools.partial(far_kernel, axes, own),
+        out_shape=pltpu.VMEM((nears, 2, pols, own, short), bf16),
+        in_specs=[vmem] * 5,
+        out_specs=vmem,
+        scratch_shapes=[
+            pltpu.VMEM((radix, LEAD, pols * CHUNK, nfft // radix), bf16),
+            pltpu.VMEM((radix, short + ROWS, LANES), jnp.float32),
+            pltpu.VMEM(tables, bf16),
+            pltpu.VMEM(tables, bf16),
+            pltpu.VMEM((pols * CHUNK // LANES, per * 2 * own, LANES), jnp.float32),
+        ],
+        compiler_params=pltpu.CompilerParams(vmem_limit_bytes=VMEM_LIMIT),
+        cost_estimate=pl.CostEstimate(
+            flops=4 * nears * own * pols * short * nfft, bytes_accessed=2 * pols * short * nfft * 2, transcendentals=0
+        ),
+        name="far",
+    )(*[pltpu.with_memory_space_constraint(x, pltpu.VMEM) for x in ready])
     brought = swap(part, half)
     part = compute("all", 0, chunks - LEAD, (devices, 2, pols, own, begin), halo)
     arrived = lax.all_to_all(part, both, split_axis=0, concat_axis=0, tiled=True)

time: 159 us -> 156 us (0.981)
  Pallas kernels: 29.9 us -> 24.5 us
  local copies, waits for them, and re-layouts: 3.6 us -> 6.74 us
    pallas_call x3 -> x2, Pallas kernels: 26.8 us -> 17.1 us  [compute(): pl.pallas_call(functools.partial(compute_kernel, axes, kind, at, own), ou...]
    unnamed x4 -> x12, local copies, waits for them, and re-layouts: 1.41 us -> 6.64 us
    pallas_call x0 -> x2, Pallas kernels: none -> 4.17 us  [the longest x1 2.72 us: local(): pl.pallas_call(functools.partial(far_kernel, axes, own), out_shape=pltpu....]
  transfers between devices with their start and end apart: 18 -> 18, of which waited for: 7 -> 7; matrix products, arithmetic and copies ran while one was open for 1% -> 0% of each run, Pallas kernels for 9% -> 5%
where the time goes in v3:
time: 156 us; the launch traced here: 154 us
  waiting for transfers between devices  95 us (61%)
  starting transfers between devices  28.1 us (18%)
  Pallas kernels  24.5 us (16%)
  local copies, waits for them, and re-layouts  6.74 us (4%)
    ppermute x16, waiting for transfers between devices, swap(): return lax.ppermute(part, both, [(i, i ^ by) for i in range(devices)])  90.3 us
    ppermute x16, starting transfers between devices, swap(): return lax.ppermute(part, both, [(i, i ^ by) for i in range(devices)])  19.5 us
    pallas_call x2, Pallas kernels, compute(): pl.pallas_call(functools.partial(compute_kernel, axes, kind, at, own), ou...  17.1 us
    unnamed x12, local copies, waits for them, and re-layouts  6.64 us
    ppermute x1, waiting for transfers between devices, local(): halo = lax.ppermute(tail, both, [(i, i + 1) for i in range(devices - 1)])  4.66 us
    all_to_all x1, starting transfers between devices, local(): lax.all_to_all(part, both, split_axis=0, concat_axis=0, tiled=True)  4.56 us
    ppermute x1, starting transfers between devices, local(): halo = lax.ppermute(tail, both, [(i, i + 1) for i in range(devices - 1)])  4.01 us
  transfers between devices with their start and end apart: 18, of which 7 were waited for; matrix products, arithmetic and copies ran while one was open for 0% of the time, Pallas kernels for 5%

profile of v3, /device:TPU:1, one launch (start us, length us, event | category | flops | bytes accessed | tf_op | source)
XLA Modules:
  0.0 154.4 jit_solution(8318126659776505556)
XLA Ops:
  0.0 1.5 prepare.1
  1.5 1.0 copy-done
  2.5 1.0 copy-done.2
  3.4 1.0 copy-done.4
  4.4 4.0 %collective-permute-start = (bf16[2,8,2048]{2,1,0:T(8,128)(2,1)S(1)}, bf16[2,8,2048]{2,1,0:T(8,128)(2,1)S(1)}, u32[]{:S(2)}, u32[]{:S(2)}) collective-permute-start(bf16[2,8,2048]{2,1,0:T(8,128)(2,1)S(1)} %get-tuple-element.11), channel_id=1, source_target_pairs={{0,1},{1,2},{2,3},{3,4},{4,5},{5,6},{6,7},{7,8},{8,9},{9,10},{10,1... | collective-permute-start | bytes 196616 | tf_op jit(solution)/shard_map/ppermute | solution.py:367
  8.4 4.7 %collective-permute-done.refs_0_ = bf16[2,8,2048]{2,1,0:T(8,128)(2,1)S(1)} collective-permute-done((bf16[2,8,2048]{2,1,0:T(8,128)(2,1)S(1)}, bf16[2,8,2048]{2,1,0:T(8,128)(2,1)S(1)}, u32[]{:S(2)}, u32[]{:S(2)}) %collective-permute-start) | collective-permute-done | bytes 65568 | tf_op jit(solution)/shard_map/ppermute | solution.py:367
  13.1 12.8 %shard_map.55 = bf16[32,2,2,32,384]{4,3,2,1,0:T(8,128)(2,1)} custom-call(bf16[2,512,2048]{2,1,0:T(8,128)(2,1)} %samples.5, bf16[2,8,2048]{2,1,0:T(8,128)(2,1)S(1)} %collective-permute-done.refs_0_, f32[8,2048]{1,0:T(8,128)} %refs_1_.3, f32[2,64,128]{2,1,0:T(8,128)} %constant.6.clone.high.refs_2_, f32[2,16,128]{2,1,0:T(8,128)} %constant.7.clone.low.refs_3_, ...), custom_call_target="tpu_custom_call" | custom-call | flops 6442450944 | bytes 6291456 | tf_op jit(solution)/shard_map/pallas_call | solution.py:318
  25.9 4.6 %all-to-all-start = ((bf16[32,2,2,32,384]{4,3,2,1,0:T(8,128)(2,1)}), bf16[32,2,2,32,384]{4,3,2,1,0:T(8,128)(2,1)S(1)}, u32[]{:S(2)}, u32[]{:S(2)}) async-start(bf16[32,2,2,32,384]{4,3,2,1,0:T(8,128)(2,1)} %shard_map.55), calls=%async_computation | async-start | bytes 6291456 | tf_op jit(solution)/shard_map/all_to_all | solution.py:388
  30.5 1.2 copy-done.1
  31.7 1.2 copy-done.3
  32.9 1.2 copy-done.5
  34.2 2.7 %far.1 = bf16[16,2,2,32,128]{4,3,2,1,0:T(8,128)(2,1)S(1)} custom-call(bf16[2,136,2048]{2,1,0:T(8,128)(2,1)S(1)} %copy-done.1, f32[8,2048]{1,0:T(8,128)S(1)} %get-tuple-element.13.taps, f32[2,8,16,128]{3,2,1,0:T(8,128)S(1)} %get-tuple-element.14.step, f32[2,1024,128]{2,1,0:T(8,128)S(1)} %copy-done.3, bf16[2,256,1024]{2,1,0:T(8,128)(2,1)S(1)} %copy-done.5), custom_call_target="tpu_custom_call" | custom-call | flops 1073741824 | bytes 2097152 | tf_op jit(solution)/shard_map/far/pallas_call | solution.py:368
  36.9 2.3 %collective-permute-start.1 = (bf16[16,2,2,32,128]{4,3,2,1,0:T(8,128)(2,1)S(1)}, bf16[16,2,2,32,128]{4,3,2,1,0:T(8,128)(2,1)S(1)}, u32[]{:S(2)}, u32[]{:S(2)}) collective-permute-start(bf16[16,2,2,32,128]{4,3,2,1,0:T(8,128)(2,1)S(1)} %far.1), channel_id=1, source_target_pairs={{0,2},{1,3},{2,0},{3,1},{4,6},{5,7},{6,4},{7,5},{8,10},{9,11},{10,... | collective-permute-start | bytes 1572872 | tf_op jit(solution)/shard_map/ppermute | solution.py:345
  39.2 85.7 %collective-permute-done.1.refs_0_ = bf16[16,2,2,32,128]{4,3,2,1,0:T(8,128)(2,1)S(1)} collective-permute-done((bf16[16,2,2,32,128]{4,3,2,1,0:T(8,128)(2,1)S(1)}, bf16[16,2,2,32,128]{4,3,2,1,0:T(8,128)(2,1)S(1)}, u32[]{:S(2)}, u32[]{:S(2)}) %collective-permute-start.1) | collective-permute-done | bytes 524320 | tf_op jit(solution)/shard_map/ppermute | solution.py:345
  124.9 4.4 %shard_map.56 = bf16[16,2,2,2,32,128]{5,4,3,2,1,0:T(8,128)(2,1)S(1)} custom-call(bf16[2,512,2048]{2,1,0:T(8,128)(2,1)} %samples.5, bf16[16,2,2,32,128]{4,3,2,1,0:T(8,128)(2,1)S(1)} %collective-permute-done.1.refs_0_, f32[8,2048]{1,0:T(8,128)} %refs_1_.3, f32[2,64,128]{2,1,0:T(8,128)} %constant.6.clone.high.refs_2_, f32[2,16,128]{2,1,0:T(8,128)} %constant.7.clone.low.refs_3_, ...), custom_call_target="tpu_custom_call" | custom-call | flops 1073741824 | bytes 2097152 | tf_op jit(solution)/shard_map/pallas_call | solution.py:318
  129.4 1.6 %collective-permute-start.15 = (bf16[2,2,2,32,128]{4,3,2,1,0:T(8,128)(2,1)S(1)}, bf16[2,2,2,32,128]{4,3,2,1,0:T(8,128)(2,1)S(1)}, u32[]{:S(2)}, u32[]{:S(2)}) collective-permute-start(bf16[2,2,2,32,128]{4,3,2,1,0:T(8,128)(2,1)S(1)} %get-tuple-element.19), channel_id=1, source_target_pairs={{0,28},{1,29},{2,30},{3,31},{4,24},{5,25},{6,26},{7,27},{8,20},{9,... | collective-permute-start | bytes 196616 | tf_op jit(solution)/shard_map/ppermute | solution.py:345
  131.1 2.6 %collective-permute-start.14 = (bf16[2,2,2,32,128]{4,3,2,1,0:T(8,128)(2,1)S(1)}, bf16[2,2,2,32,128]{4,3,2,1,0:T(8,128)(2,1)S(1)}, u32[]{:S(2)}, u32[]{:S(2)}) collective-permute-start(bf16[2,2,2,32,128]{4,3,2,1,0:T(8,128)(2,1)S(1)} %get-tuple-element.20), channel_id=1, source_target_pairs={{0,25},{1,24},{2,27},{3,26},{4,29},{5,28},{6,31},{7,30},{8,17},{9,... | collective-permute-start | bytes 196616 | tf_op jit(solution)/shard_map/ppermute | solution.py:345
  133.7 1.6 %collective-permute-start.13 = (bf16[2,2,2,32,128]{4,3,2,1,0:T(8,128)(2,1)S(1)}, bf16[2,2,2,32,128]{4,3,2,1,0:T(8,128)(2,1)S(1)}, u32[]{:S(2)}, u32[]{:S(2)}) collective-permute-start(bf16[2,2,2,32,128]{4,3,2,1,0:T(8,128)(2,1)S(1)} %get-tuple-element.21), channel_id=1, source_target_pairs={{0,24},{1,25},{2,26},{3,27},{4,28},{5,29},{6,30},{7,31},{8,16},{9,... | collective-permute-start | bytes 196616 | tf_op jit(solution)/shard_map/ppermute | solution.py:345
  135.7 2.3 %collective-permute-start.11 = (bf16[2,2,2,32,128]{4,3,2,1,0:T(8,128)(2,1)S(1)}, bf16[2,2,2,32,128]{4,3,2,1,0:T(8,128)(2,1)S(1)}, u32[]{:S(2)}, u32[]{:S(2)}) collective-permute-start(bf16[2,2,2,32,128]{4,3,2,1,0:T(8,128)(2,1)S(1)} %get-tuple-element.23), channel_id=1, source_target_pairs={{0,20},{1,21},{2,22},{3,23},{4,16},{5,17},{6,18},{7,19},{8,28},{9,... | collective-permute-start | bytes 196616 | tf_op jit(solution)/shard_map/ppermute | solution.py:345
  138.0 1.2 collective-permute-start.10
  139.2 1.2 collective-permute-start.9
  140.4 1.5 collective-permute-start.8
  141.9 0.6 collective-permute-start.7
  142.5 1.4 collective-permute-done.11.refs_9_
  143.9 1.0 collective-permute-start.6
  144.9 0.9 collective-permute-start.5
  145.8 2.2 %collective-permute-start.4 = (bf16[2,2,2,32,128]{4,3,2,1,0:T(8,128)(2,1)S(1)}, bf16[2,2,2,32,128]{4,3,2,1,0:T(8,128)(2,1)S(1)}, u32[]{:S(2)}, u32[]{:S(2)}) collective-permute-start(bf16[2,2,2,32,128]{4,3,2,1,0:T(8,128)(2,1)S(1)} %get-tuple-element.30), channel_id=1, source_target_pairs={{0,5},{1,4},{2,7},{3,6},{4,1},{5,0},{6,3},{7,2},{8,13},{9,12},{10,... | collective-permute-start | bytes 196616 | tf_op jit(solution)/shard_map/ppermute | solution.py:345
  148.2 1.6 %collective-permute-done.5.refs_3_ = bf16[2,2,2,32,128]{4,3,2,1,0:T(8,128)(2,1)S(1)} collective-permute-done((bf16[2,2,2,32,128]{4,3,2,1,0:T(8,128)(2,1)S(1)}, bf16[2,2,2,32,128]{4,3,2,1,0:T(8,128)(2,1)S(1)}, u32[]{:S(2)}, u32[]{:S(2)}) %collective-permute-start.5) | collective-permute-done | bytes 65568 | tf_op jit(solution)/shard_map/ppermute | solution.py:345
  149.8 0.5 collective-permute-done.4.refs_2_
  150.2 0.9 collective-permute-done.2.refs_0_
  151.2 1.2 place_near.1.held
  152.4 1.9 %place_main.1 = bf16[2,2,32,16384]{3,2,1,0:T(8,128)(2,1)} custom-call(bf16[32,2,2,32,384]{4,3,2,1,0:T(8,128)(2,1)S(1)} %all-to-all-done.block, bf16[2,2,32,16384]{3,2,1,0:T(8,128)(2,1)} %place_near.1.held), custom_call_target="tpu_custom_call", output_to_operand_aliasing={{}: (1, {})} | custom-call | tf_op jit(solution)/shard_map/place_main/pallas_call | solution.py:400
  (23 shorter events, 0.7 us)
Async XLA Ops:
  1.5 1.0 copy-start
  2.5 1.0 copy-start.2
  3.4 1.0 copy-start.4
  4.4 8.7 %collective-permute-start = (bf16[2,8,2048]{2,1,0:T(8,128)(2,1)S(1)}, bf16[2,8,2048]{2,1,0:T(8,128)(2,1)S(1)}, u32[]{:S(2)}, u32[]{:S(2)}) collective-permute-start(bf16[2,8,2048]{2,1,0:T(8,128)(2,1)S(1)} %get-tuple-element.11), channel_id=1, source_target_pairs={{0,1},{1,2},{2,3},{3,4},{4,5},{5,6},{6,7},{7,8},{8,9},{9,10},{10,1... | collective-permute-start | bytes 196616 | tf_op jit(solution)/shard_map/ppermute | solution.py:367
  25.9 126.5 %all-to-all-start = ((bf16[32,2,2,32,384]{4,3,2,1,0:T(8,128)(2,1)}), bf16[32,2,2,32,384]{4,3,2,1,0:T(8,128)(2,1)S(1)}, u32[]{:S(2)}, u32[]{:S(2)}) async-start(bf16[32,2,2,32,384]{4,3,2,1,0:T(8,128)(2,1)} %shard_map.55), calls=%async_computation | async-start | bytes 6291456 | tf_op jit(solution)/shard_map/all_to_all | solution.py:388
  30.5 1.3 copy-start.1
  31.7 1.2 copy-start.3
  32.9 1.2 copy-start.5
  36.9 88.0 %collective-permute-start.1 = (bf16[16,2,2,32,128]{4,3,2,1,0:T(8,128)(2,1)S(1)}, bf16[16,2,2,32,128]{4,3,2,1,0:T(8,128)(2,1)S(1)}, u32[]{:S(2)}, u32[]{:S(2)}) collective-permute-start(bf16[16,2,2,32,128]{4,3,2,1,0:T(8,128)(2,1)S(1)} %far.1), channel_id=1, source_target_pairs={{0,2},{1,3},{2,0},{3,1},{4,6},{5,7},{6,4},{7,5},{8,10},{9,11},{10,... | collective-permute-start | bytes 1572872 | tf_op jit(solution)/shard_map/ppermute | solution.py:345
  129.4 6.3 %collective-permute-start.16 = (bf16[2,2,2,32,128]{4,3,2,1,0:T(8,128)(2,1)S(1)}, bf16[2,2,2,32,128]{4,3,2,1,0:T(8,128)(2,1)S(1)}, u32[]{:S(2)}, u32[]{:S(2)}) collective-permute-start(bf16[2,2,2,32,128]{4,3,2,1,0:T(8,128)(2,1)S(1)} %get-tuple-element.18), channel_id=1, source_target_pairs={{0,29},{1,28},{2,31},{3,30},{4,25},{5,24},{6,27},{7,26},{8,21},{9,... | collective-permute-start | bytes 196616 | tf_op jit(solution)/shard_map/ppermute | solution.py:345
  129.4 8.5 %collective-permute-start.15 = (bf16[2,2,2,32,128]{4,3,2,1,0:T(8,128)(2,1)S(1)}, bf16[2,2,2,32,128]{4,3,2,1,0:T(8,128)(2,1)S(1)}, u32[]{:S(2)}, u32[]{:S(2)}) collective-permute-start(bf16[2,2,2,32,128]{4,3,2,1,0:T(8,128)(2,1)S(1)} %get-tuple-element.19), channel_id=1, source_target_pairs={{0,28},{1,29},{2,30},{3,31},{4,24},{5,25},{6,26},{7,27},{8,20},{9,... | collective-permute-start | bytes 196616 | tf_op jit(solution)/shard_map/ppermute | solution.py:345
  131.1 8.1 %collective-permute-start.14 = (bf16[2,2,2,32,128]{4,3,2,1,0:T(8,128)(2,1)S(1)}, bf16[2,2,2,32,128]{4,3,2,1,0:T(8,128)(2,1)S(1)}, u32[]{:S(2)}, u32[]{:S(2)}) collective-permute-start(bf16[2,2,2,32,128]{4,3,2,1,0:T(8,128)(2,1)S(1)} %get-tuple-element.20), channel_id=1, source_target_pairs={{0,25},{1,24},{2,27},{3,26},{4,29},{5,28},{6,31},{7,30},{8,17},{9,... | collective-permute-start | bytes 196616 | tf_op jit(solution)/shard_map/ppermute | solution.py:345
  133.7 6.7 %collective-permute-start.13 = (bf16[2,2,2,32,128]{4,3,2,1,0:T(8,128)(2,1)S(1)}, bf16[2,2,2,32,128]{4,3,2,1,0:T(8,128)(2,1)S(1)}, u32[]{:S(2)}, u32[]{:S(2)}) collective-permute-start(bf16[2,2,2,32,128]{4,3,2,1,0:T(8,128)(2,1)S(1)} %get-tuple-element.21), channel_id=1, source_target_pairs={{0,24},{1,25},{2,26},{3,27},{4,28},{5,29},{6,30},{7,31},{8,16},{9,... | collective-permute-start | bytes 196616 | tf_op jit(solution)/shard_map/ppermute | solution.py:345
  135.3 6.6 %collective-permute-start.12 = (bf16[2,2,2,32,128]{4,3,2,1,0:T(8,128)(2,1)S(1)}, bf16[2,2,2,32,128]{4,3,2,1,0:T(8,128)(2,1)S(1)}, u32[]{:S(2)}, u32[]{:S(2)}) collective-permute-start(bf16[2,2,2,32,128]{4,3,2,1,0:T(8,128)(2,1)S(1)} %get-tuple-element.22), channel_id=1, source_target_pairs={{0,21},{1,20},{2,23},{3,22},{4,17},{5,16},{6,19},{7,18},{8,29},{9,... | collective-permute-start | bytes 196616 | tf_op jit(solution)/shard_map/ppermute | solution.py:345
  135.7 8.3 %collective-permute-start.11 = (bf16[2,2,2,32,128]{4,3,2,1,0:T(8,128)(2,1)S(1)}, bf16[2,2,2,32,128]{4,3,2,1,0:T(8,128)(2,1)S(1)}, u32[]{:S(2)}, u32[]{:S(2)}) collective-permute-start(bf16[2,2,2,32,128]{4,3,2,1,0:T(8,128)(2,1)S(1)} %get-tuple-element.23), channel_id=1, source_target_pairs={{0,20},{1,21},{2,22},{3,23},{4,16},{5,17},{6,18},{7,19},{8,28},{9,... | collective-permute-start | bytes 196616 | tf_op jit(solution)/shard_map/ppermute | solution.py:345
  138.0 7.0 %collective-permute-start.10 = (bf16[2,2,2,32,128]{4,3,2,1,0:T(8,128)(2,1)S(1)}, bf16[2,2,2,32,128]{4,3,2,1,0:T(8,128)(2,1)S(1)}, u32[]{:S(2)}, u32[]{:S(2)}) collective-permute-start(bf16[2,2,2,32,128]{4,3,2,1,0:T(8,128)(2,1)S(1)} %get-tuple-element.24), channel_id=1, source_target_pairs={{0,17},{1,16},{2,19},{3,18},{4,21},{5,20},{6,23},{7,22},{8,25},{9,... | collective-permute-start | bytes 196616 | tf_op jit(solution)/shard_map/ppermute | solution.py:345
  139.2 6.6 %collective-permute-start.9 = (bf16[2,2,2,32,128]{4,3,2,1,0:T(8,128)(2,1)S(1)}, bf16[2,2,2,32,128]{4,3,2,1,0:T(8,128)(2,1)S(1)}, u32[]{:S(2)}, u32[]{:S(2)}) collective-permute-start(bf16[2,2,2,32,128]{4,3,2,1,0:T(8,128)(2,1)S(1)} %get-tuple-element.25), channel_id=1, source_target_pairs={{0,16},{1,17},{2,18},{3,19},{4,20},{5,21},{6,22},{7,23},{8,24},{9,... | collective-permute-start | bytes 196616 | tf_op jit(solution)/shard_map/ppermute | solution.py:345
  140.4 7.6 %collective-permute-start.8 = (bf16[2,2,2,32,128]{4,3,2,1,0:T(8,128)(2,1)S(1)}, bf16[2,2,2,32,128]{4,3,2,1,0:T(8,128)(2,1)S(1)}, u32[]{:S(2)}, u32[]{:S(2)}) collective-permute-start(bf16[2,2,2,32,128]{4,3,2,1,0:T(8,128)(2,1)S(1)} %get-tuple-element.26), channel_id=1, source_target_pairs={{0,13},{1,12},{2,15},{3,14},{4,9},{5,8},{6,11},{7,10},{8,5},{9,4},... | collective-permute-start | bytes 196616 | tf_op jit(solution)/shard_map/ppermute | solution.py:345
  141.9 6.1 %collective-permute-start.7 = (bf16[2,2,2,32,128]{4,3,2,1,0:T(8,128)(2,1)S(1)}, bf16[2,2,2,32,128]{4,3,2,1,0:T(8,128)(2,1)S(1)}, u32[]{:S(2)}, u32[]{:S(2)}) collective-permute-start(bf16[2,2,2,32,128]{4,3,2,1,0:T(8,128)(2,1)S(1)} %get-tuple-element.27), channel_id=1, source_target_pairs={{0,12},{1,13},{2,14},{3,15},{4,8},{5,9},{6,10},{7,11},{8,4},{9,5},... | collective-permute-start | bytes 196616 | tf_op jit(solution)/shard_map/ppermute | solution.py:345
  143.9 4.3 %collective-permute-start.6 = (bf16[2,2,2,32,128]{4,3,2,1,0:T(8,128)(2,1)S(1)}, bf16[2,2,2,32,128]{4,3,2,1,0:T(8,128)(2,1)S(1)}, u32[]{:S(2)}, u32[]{:S(2)}) collective-permute-start(bf16[2,2,2,32,128]{4,3,2,1,0:T(8,128)(2,1)S(1)} %get-tuple-element.28), channel_id=1, source_target_pairs={{0,9},{1,8},{2,11},{3,10},{4,13},{5,12},{6,15},{7,14},{8,1},{9,0},... | collective-permute-start | bytes 196616 | tf_op jit(solution)/shard_map/ppermute | solution.py:345
  144.9 4.9 %collective-permute-start.5 = (bf16[2,2,2,32,128]{4,3,2,1,0:T(8,128)(2,1)S(1)}, bf16[2,2,2,32,128]{4,3,2,1,0:T(8,128)(2,1)S(1)}, u32[]{:S(2)}, u32[]{:S(2)}) collective-permute-start(bf16[2,2,2,32,128]{4,3,2,1,0:T(8,128)(2,1)S(1)} %get-tuple-element.29), channel_id=1, source_target_pairs={{0,8},{1,9},{2,10},{3,11},{4,12},{5,13},{6,14},{7,15},{8,0},{9,1},... | collective-permute-start | bytes 196616 | tf_op jit(solution)/shard_map/ppermute | solution.py:345
  145.8 4.4 %collective-permute-start.4 = (bf16[2,2,2,32,128]{4,3,2,1,0:T(8,128)(2,1)S(1)}, bf16[2,2,2,32,128]{4,3,2,1,0:T(8,128)(2,1)S(1)}, u32[]{:S(2)}, u32[]{:S(2)}) collective-permute-start(bf16[2,2,2,32,128]{4,3,2,1,0:T(8,128)(2,1)S(1)} %get-tuple-element.30), channel_id=1, source_target_pairs={{0,5},{1,4},{2,7},{3,6},{4,1},{5,0},{6,3},{7,2},{8,13},{9,12},{10,... | collective-permute-start | bytes 196616 | tf_op jit(solution)/shard_map/ppermute | solution.py:345
  148.0 2.2 %collective-permute-start.3 = (bf16[2,2,2,32,128]{4,3,2,1,0:T(8,128)(2,1)S(1)}, bf16[2,2,2,32,128]{4,3,2,1,0:T(8,128)(2,1)S(1)}, u32[]{:S(2)}, u32[]{:S(2)}) collective-permute-start(bf16[2,2,2,32,128]{4,3,2,1,0:T(8,128)(2,1)S(1)} %get-tuple-element.31), channel_id=1, source_target_pairs={{0,4},{1,5},{2,6},{3,7},{4,0},{5,1},{6,2},{7,3},{8,12},{9,13},{10,... | collective-permute-start | bytes 196616 | tf_op jit(solution)/shard_map/ppermute | solution.py:345
  148.0 3.2 %collective-permute-start.2 = (bf16[2,2,2,32,128]{4,3,2,1,0:T(8,128)(2,1)S(1)}, bf16[2,2,2,32,128]{4,3,2,1,0:T(8,128)(2,1)S(1)}, u32[]{:S(2)}, u32[]{:S(2)}) collective-permute-start(bf16[2,2,2,32,128]{4,3,2,1,0:T(8,128)(2,1)S(1)} %get-tuple-element.32), channel_id=1, source_target_pairs={{0,1},{1,0},{2,3},{3,2},{4,5},{5,4},{6,7},{7,6},{8,9},{9,8},{10,11... | collective-permute-start | bytes 196616 | tf_op jit(solution)/shard_map/ppermute | solution.py:345

commit v4 on v3

--- a/solution.py
+++ b/solution.py
@@ -41,31 +41,31 @@
     rows = 64 // radix
 
     def body(step, carry):
-        pol = lax.rem(step, pols)
-        lane = pl.multiple_of(step // pols * LANES, LANES)
+        lane = pl.multiple_of(step * LANES, LANES)
         taps = []
         for part in range(radix):
             at = pl.ds(lane + part * width, LANES)
-            load(step, pol, part, at)
+            load(step, part, at)
             taps.append(taps_ref[:, at])
         for chunk in range(chunks):
             for first in range(0, CHUNK, rows):
-                totals = []
-                for part in range(radix):
-                    total = None
-                    for tap in range(tap_count):
-                        start = ROWS + chunk * CHUNK + first + tap - (tap_count - 1)
-                        term = taps[part][tap : tap + 1, :] * ext_ref[part, pl.ds(start, rows), :]
-                        total = term if total is None else total + term
-                    totals.append(total)
-                to = pl.ds(pl.multiple_of(pol * CHUNK + first, rows), rows)
-                if radix == 2:
-                    totals = [totals[0] + totals[1], totals[0] - totals[1]]
-                for part in range(radix):
-                    weighted_ref[part, chunk, to, pl.ds(lane, LANES)] = totals[part].astype(jnp.bfloat16)
+                for pol in range(pols):
+                    totals = []
+                    for part in range(radix):
+                        total = None
+                        for tap in range(tap_count):
+                            start = ROWS + chunk * CHUNK + first + tap - (tap_count - 1)
+                            term = taps[part][tap : tap + 1, :] * ext_ref[pol, part, pl.ds(start, rows), :]
+                            total = term if total is None else total + term
+                        totals.append(total)
+                    to = pl.ds(pol * CHUNK + first, rows)
+                    if radix == 2:
+                        totals = [totals[0] + totals[1], totals[0] - totals[1]]
+                    for part in range(radix):
+                        weighted_ref[part, chunk, to, pl.ds(lane, LANES)] = totals[part].astype(jnp.bfloat16)
         return carry
 
-    lax.fori_loop(0, pols * width // LANES, body, 0)
+    lax.fori_loop(0, width // LANES, body, 0)
 
 
 def fill_phases(high_ref, low_ref, phase_ref):
@@ -168,17 +168,17 @@
         copy.wait()
     fill_phases(high_in, low_in, phase)
     me = position(axes)
-    fill_table(0, lambda item: me ^ (within(axes, item) + axes[1][1] // 2), own, phase, step_out, table)
+    fill_table(0, lambda item: me ^ (within(axes, item) ^ (axes[1][1] - 1)), own, phase, step_out, table)
     for copy in copies[3:]:
         copy.wait()
 
 
 def far_kernel(axes, own, rows, taps, step, phase, table, out, weighted, ext, table_next, table_spare, mixed):
     me = position(axes)
-    dest_of = lambda item: me ^ (within(axes, item) + axes[1][1] // 2)
-
-    def load(at_step, pol, part, at):
-        ext[part] = rows[pol, :, at].astype(jnp.float32)
+    dest_of = lambda item: me ^ (within(axes, item) ^ (axes[1][1] - 1))
+
+    def load(at_step, part, at):
+        ext[:, part] = rows[:, :, at].astype(jnp.float32)
 
     def store(item, c, chunk, part):
         for pol in range(out.shape[2]):
@@ -242,16 +242,16 @@
         copy.wait()
     fill_phases(high, low, phase)
     fill_table(0, dest_of, own, phase, step, table)
-    steps = wide // LANES * pols
-
-    def load(at_step, pol, part, at):
+    steps = wide // LANES
+
+    def load(at_step, part, at):
         for piece in range(pieces):
             pl.when(at_step == piece * steps)(copies[piece * radix + part].wait)
         if halo is not None:
-            ext[part, pl.ds(0, ROWS), :] = halo[pol, :, at].astype(jnp.float32)
-            ext[part, pl.ds(ROWS, held), :] = rows[pol, :, at].astype(jnp.float32)
+            ext[:, part, pl.ds(0, ROWS), :] = halo[:, :, at].astype(jnp.float32)
+            ext[:, part, pl.ds(ROWS, held), :] = rows[:, :, at].astype(jnp.float32)
         else:
-            ext[part] = rows[pol, :, at].astype(jnp.float32)
+            ext[:, part] = rows[:, :, at].astype(jnp.float32)
 
     fir(load, count // CHUNK, taps, weighted, ext)
     transform(store, out.shape[0], dest_of, own, weighted, phase, step, (table, table_next), mixed)
@@ -270,13 +270,12 @@
 
 def place_near_kernel(axes, frames, begin, *refs):
     blocks, (mine, out, sems) = refs[:-3], refs[-3:]
-    half = axes[1][1] // 2
     me = position(axes)
     copies = []
     for item in range(len(blocks) + 1):
         block = mine if item == 0 else blocks[item - 1]
         for side in range(2):
-            source = me ^ (within(axes, item) + side * half)
+            source = me ^ (within(axes, item) ^ (side * (axes[1][1] - 1)))
             at = pl.ds(pl.multiple_of(source * frames + begin, CHUNK), frames - begin)
             copies.append(pltpu.make_async_copy(block.at[side], out.at[:, :, :, at], sems.at[2 * item + side]))
     for copy in copies:
@@ -323,7 +322,7 @@
             scratch_shapes=[
                 pltpu.VMEM((pols, held, nfft), bf16),
                 pltpu.VMEM((radix, count, pols * CHUNK, nfft // radix), bf16),
-                pltpu.VMEM((radix, count * CHUNK + ROWS, LANES), jnp.float32),
+                pltpu.VMEM((pols, radix, count * CHUNK + ROWS, LANES), jnp.float32),
                 pltpu.VMEM((2, channels, LANES), jnp.float32),
                 pltpu.VMEM((radix, per * 2 * own // radix, nfft // radix), bf16),
                 pltpu.VMEM((radix, per * 2 * own // radix, nfft // radix), bf16),
@@ -372,7 +371,7 @@
         out_specs=vmem,
         scratch_shapes=[
             pltpu.VMEM((radix, LEAD, pols * CHUNK, nfft // radix), bf16),
-            pltpu.VMEM((radix, short + ROWS, LANES), jnp.float32),
+            pltpu.VMEM((pols, radix, short + ROWS, LANES), jnp.float32),
             pltpu.VMEM(tables, bf16),
             pltpu.VMEM(tables, bf16),
             pltpu.VMEM((pols * CHUNK // LANES, per * 2 * own, LANES), jnp.float32),
@@ -383,7 +382,7 @@
         ),
         name="far",
     )(*[pltpu.with_memory_space_constraint(x, pltpu.VMEM) for x in ready])
-    brought = swap(part, half)
+    brought = swap(part, column_count - 1)
     part = compute("all", 0, chunks - LEAD, (devices, 2, pols, own, begin), halo)
     arrived = lax.all_to_all(part, both, split_axis=0, concat_axis=0, tiled=True)
     part = compute("near", begin, LEAD, (nears, 2, 2, pols, own, short), brought)

time: 156 us -> 155 us (level)
  starting transfers between devices: 28.1 us -> 57.1 us
  waiting for transfers between devices: 95 us -> 66.4 us
    ppermute x16, starting transfers between devices: 19.5 us -> 48.6 us  [swap(): return lax.ppermute(part, both, [(i, i ^ by) for i in range(devices)])]
    ppermute x16, waiting for transfers between devices: 90.3 us -> 61.8 us  [swap(): return lax.ppermute(part, both, [(i, i ^ by) for i in range(devices)])]
  transfers between devices with their start and end apart: 18 -> 18, of which waited for: 7 -> 5; matrix products, arithmetic and copies ran while one was open for 0% -> 0% of each run, Pallas kernels for 5% -> 5%
where the time goes in v4:
time: 155 us; the launch traced here: 154 us
  waiting for transfers between devices  66.4 us (43%)
  starting transfers between devices  57.1 us (37%)
  Pallas kernels  23.8 us (15%)
  local copies, waits for them, and re-layouts  6.74 us (4%)
    ppermute x16, waiting for transfers between devices, swap(): return lax.ppermute(part, both, [(i, i ^ by) for i in range(devices)])  61.8 us
    ppermute x16, starting transfers between devices, swap(): return lax.ppermute(part, both, [(i, i ^ by) for i in range(devices)])  48.6 us
    pallas_call x2, Pallas kernels, compute(): pl.pallas_call(functools.partial(compute_kernel, axes, kind, at, own), ou...  16.6 us
    unnamed x12, local copies, waits for them, and re-layouts  6.64 us
    ppermute x1, waiting for transfers between devices, local(): halo = lax.ppermute(tail, both, [(i, i + 1) for i in range(devices - 1)])  4.66 us
    all_to_all x1, starting transfers between devices, local(): lax.all_to_all(part, both, split_axis=0, concat_axis=0, tiled=True)  4.56 us
    ppermute x1, starting transfers between devices, local(): halo = lax.ppermute(tail, both, [(i, i + 1) for i in range(devices - 1)])  4.01 us
  transfers between devices with their start and end apart: 18, of which 5 were waited for; matrix products, arithmetic and copies ran while one was open for 0% of the time, Pallas kernels for 5%

profile of v4, /device:TPU:1, one launch (start us, length us, event | category | flops | bytes accessed | tf_op | source)
XLA Modules:
  0.0 154.2 jit_solution(6405991999320713278)
XLA Ops:
  0.0 1.5 prepare.1
  1.5 1.0 copy-done
  2.5 1.0 copy-done.2
  3.4 1.0 copy-done.4
  4.4 4.0 %collective-permute-start = (bf16[2,8,2048]{2,1,0:T(8,128)(2,1)S(1)}, bf16[2,8,2048]{2,1,0:T(8,128)(2,1)S(1)}, u32[]{:S(2)}, u32[]{:S(2)}) collective-permute-start(bf16[2,8,2048]{2,1,0:T(8,128)(2,1)S(1)} %get-tuple-element.11), channel_id=1, source_target_pairs={{0,1},{1,2},{2,3},{3,4},{4,5},{5,6},{6,7},{7,8},{8,9},{9,10},{10,1... | collective-permute-start | bytes 196616 | tf_op jit(solution)/shard_map/ppermute | solution.py:366
  8.4 4.7 %collective-permute-done.refs_0_ = bf16[2,8,2048]{2,1,0:T(8,128)(2,1)S(1)} collective-permute-done((bf16[2,8,2048]{2,1,0:T(8,128)(2,1)S(1)}, bf16[2,8,2048]{2,1,0:T(8,128)(2,1)S(1)}, u32[]{:S(2)}, u32[]{:S(2)}) %collective-permute-start) | collective-permute-done | bytes 65568 | tf_op jit(solution)/shard_map/ppermute | solution.py:366
  13.1 12.5 %shard_map.55 = bf16[32,2,2,32,384]{4,3,2,1,0:T(8,128)(2,1)} custom-call(bf16[2,512,2048]{2,1,0:T(8,128)(2,1)} %samples.5, bf16[2,8,2048]{2,1,0:T(8,128)(2,1)S(1)} %collective-permute-done.refs_0_, f32[8,2048]{1,0:T(8,128)} %refs_1_.3, f32[2,64,128]{2,1,0:T(8,128)} %constant.6.clone.high.refs_2_, f32[2,16,128]{2,1,0:T(8,128)} %constant.7.clone.low.refs_3_, ...), custom_call_target="tpu_custom_call" | custom-call | flops 6442450944 | bytes 6291456 | tf_op jit(solution)/shard_map/pallas_call | solution.py:317
  25.6 4.6 %all-to-all-start = ((bf16[32,2,2,32,384]{4,3,2,1,0:T(8,128)(2,1)}), bf16[32,2,2,32,384]{4,3,2,1,0:T(8,128)(2,1)S(1)}, u32[]{:S(2)}, u32[]{:S(2)}) async-start(bf16[32,2,2,32,384]{4,3,2,1,0:T(8,128)(2,1)} %shard_map.55), calls=%async_computation | async-start | bytes 6291456 | tf_op jit(solution)/shard_map/all_to_all | solution.py:387
  30.2 1.2 copy-done.1
  31.4 1.2 copy-done.3
  32.6 1.2 copy-done.5
  33.9 2.6 %far.1 = bf16[16,2,2,32,128]{4,3,2,1,0:T(8,128)(2,1)S(1)} custom-call(bf16[2,136,2048]{2,1,0:T(8,128)(2,1)S(1)} %copy-done.1, f32[8,2048]{1,0:T(8,128)S(1)} %get-tuple-element.13.taps, f32[2,8,16,128]{3,2,1,0:T(8,128)S(1)} %get-tuple-element.14.step, f32[2,1024,128]{2,1,0:T(8,128)S(1)} %copy-done.3, bf16[2,256,1024]{2,1,0:T(8,128)(2,1)S(1)} %copy-done.5), custom_call_target="tpu_custom_call" | custom-call | flops 1073741824 | bytes 2097152 | tf_op jit(solution)/shard_map/far/pallas_call | solution.py:367
  36.4 3.3 %collective-permute-start.1 = (bf16[16,2,2,32,128]{4,3,2,1,0:T(8,128)(2,1)S(1)}, bf16[16,2,2,32,128]{4,3,2,1,0:T(8,128)(2,1)S(1)}, u32[]{:S(2)}, u32[]{:S(2)}) collective-permute-start(bf16[16,2,2,32,128]{4,3,2,1,0:T(8,128)(2,1)S(1)} %far.1), channel_id=1, source_target_pairs={{0,3},{1,2},{2,1},{3,0},{4,7},{5,6},{6,5},{7,4},{8,11},{9,10},{10,... | collective-permute-start | bytes 1572872 | tf_op jit(solution)/shard_map/ppermute | solution.py:344
  39.7 57.4 %collective-permute-done.1.refs_0_ = bf16[16,2,2,32,128]{4,3,2,1,0:T(8,128)(2,1)S(1)} collective-permute-done((bf16[16,2,2,32,128]{4,3,2,1,0:T(8,128)(2,1)S(1)}, bf16[16,2,2,32,128]{4,3,2,1,0:T(8,128)(2,1)S(1)}, u32[]{:S(2)}, u32[]{:S(2)}) %collective-permute-start.1) | collective-permute-done | bytes 524320 | tf_op jit(solution)/shard_map/ppermute | solution.py:344
  97.1 4.1 %shard_map.56 = bf16[16,2,2,2,32,128]{5,4,3,2,1,0:T(8,128)(2,1)S(1)} custom-call(bf16[2,512,2048]{2,1,0:T(8,128)(2,1)} %samples.5, bf16[16,2,2,32,128]{4,3,2,1,0:T(8,128)(2,1)S(1)} %collective-permute-done.1.refs_0_, f32[8,2048]{1,0:T(8,128)} %refs_1_.3, f32[2,64,128]{2,1,0:T(8,128)} %constant.6.clone.high.refs_2_, f32[2,16,128]{2,1,0:T(8,128)} %constant.7.clone.low.refs_3_, ...), custom_call_target="tpu_custom_call" | custom-call | flops 1073741824 | bytes 2097152 | tf_op jit(solution)/shard_map/pallas_call | solution.py:317
  101.4 29.1 %collective-permute-start.16 = (bf16[2,2,2,32,128]{4,3,2,1,0:T(8,128)(2,1)S(1)}, bf16[2,2,2,32,128]{4,3,2,1,0:T(8,128)(2,1)S(1)}, u32[]{:S(2)}, u32[]{:S(2)}) collective-permute-start(bf16[2,2,2,32,128]{4,3,2,1,0:T(8,128)(2,1)S(1)} %get-tuple-element.18), channel_id=1, source_target_pairs={{0,29},{1,28},{2,31},{3,30},{4,25},{5,24},{6,27},{7,26},{8,21},{9,... | collective-permute-start | bytes 196616 | tf_op jit(solution)/shard_map/ppermute | solution.py:344
  130.5 1.1 collective-permute-start.15
  131.5 0.7 collective-permute-start.14
  132.2 0.7 collective-permute-start.13
  132.9 4.5 %collective-permute-start.12 = (bf16[2,2,2,32,128]{4,3,2,1,0:T(8,128)(2,1)S(1)}, bf16[2,2,2,32,128]{4,3,2,1,0:T(8,128)(2,1)S(1)}, u32[]{:S(2)}, u32[]{:S(2)}) collective-permute-start(bf16[2,2,2,32,128]{4,3,2,1,0:T(8,128)(2,1)S(1)} %get-tuple-element.22), channel_id=1, source_target_pairs={{0,21},{1,20},{2,23},{3,22},{4,17},{5,16},{6,19},{7,18},{8,29},{9,... | collective-permute-start | bytes 196616 | tf_op jit(solution)/shard_map/ppermute | solution.py:344
  137.4 0.9 collective-permute-start.10
  138.3 0.6 collective-permute-start.9
  138.9 2.9 %collective-permute-start.8 = (bf16[2,2,2,32,128]{4,3,2,1,0:T(8,128)(2,1)S(1)}, bf16[2,2,2,32,128]{4,3,2,1,0:T(8,128)(2,1)S(1)}, u32[]{:S(2)}, u32[]{:S(2)}) collective-permute-start(bf16[2,2,2,32,128]{4,3,2,1,0:T(8,128)(2,1)S(1)} %get-tuple-element.26), channel_id=1, source_target_pairs={{0,13},{1,12},{2,15},{3,14},{4,9},{5,8},{6,11},{7,10},{8,5},{9,4},... | collective-permute-start | bytes 196616 | tf_op jit(solution)/shard_map/ppermute | solution.py:344
  141.8 1.1 collective-permute-done.11.refs_9_
  142.9 1.2 collective-permute-start.6
  144.1 0.7 collective-permute-start.5
  144.9 1.0 collective-permute-start.4
  146.5 1.4 collective-permute-start.2
  147.8 1.4 collective-permute-done.5.refs_3_
  149.3 1.8 %collective-permute-done.2.refs_0_ = bf16[2,2,2,32,128]{4,3,2,1,0:T(8,128)(2,1)S(1)} collective-permute-done((bf16[2,2,2,32,128]{4,3,2,1,0:T(8,128)(2,1)S(1)}, bf16[2,2,2,32,128]{4,3,2,1,0:T(8,128)(2,1)S(1)}, u32[]{:S(2)}, u32[]{:S(2)}) %collective-permute-start.2) | collective-permute-done | bytes 65568 | tf_op jit(solution)/shard_map/ppermute | solution.py:344
  151.1 1.2 place_near.1.held
  152.3 1.9 %place_main.1 = bf16[2,2,32,16384]{3,2,1,0:T(8,128)(2,1)} custom-call(bf16[32,2,2,32,384]{4,3,2,1,0:T(8,128)(2,1)S(1)} %all-to-all-done.block, bf16[2,2,32,16384]{3,2,1,0:T(8,128)(2,1)} %place_near.1.held), custom_call_target="tpu_custom_call", output_to_operand_aliasing={{}: (1, {})} | custom-call | tf_op jit(solution)/shard_map/place_main/pallas_call | solution.py:399
  (23 shorter events, 0.8 us)
Async XLA Ops:
  1.5 1.0 copy-start
  2.5 1.0 copy-start.2
  3.4 1.0 copy-start.4
  4.4 8.7 %collective-permute-start = (bf16[2,8,2048]{2,1,0:T(8,128)(2,1)S(1)}, bf16[2,8,2048]{2,1,0:T(8,128)(2,1)S(1)}, u32[]{:S(2)}, u32[]{:S(2)}) collective-permute-start(bf16[2,8,2048]{2,1,0:T(8,128)(2,1)S(1)} %get-tuple-element.11), channel_id=1, source_target_pairs={{0,1},{1,2},{2,3},{3,4},{4,5},{5,6},{6,7},{7,8},{8,9},{9,10},{10,1... | collective-permute-start | bytes 196616 | tf_op jit(solution)/shard_map/ppermute | solution.py:366
  25.6 126.7 %all-to-all-start = ((bf16[32,2,2,32,384]{4,3,2,1,0:T(8,128)(2,1)}), bf16[32,2,2,32,384]{4,3,2,1,0:T(8,128)(2,1)S(1)}, u32[]{:S(2)}, u32[]{:S(2)}) async-start(bf16[32,2,2,32,384]{4,3,2,1,0:T(8,128)(2,1)} %shard_map.55), calls=%async_computation | async-start | bytes 6291456 | tf_op jit(solution)/shard_map/all_to_all | solution.py:387
  30.1 1.3 copy-start.1
  31.4 1.2 copy-start.3
  32.6 1.2 copy-start.5
  36.4 60.7 %collective-permute-start.1 = (bf16[16,2,2,32,128]{4,3,2,1,0:T(8,128)(2,1)S(1)}, bf16[16,2,2,32,128]{4,3,2,1,0:T(8,128)(2,1)S(1)}, u32[]{:S(2)}, u32[]{:S(2)}) collective-permute-start(bf16[16,2,2,32,128]{4,3,2,1,0:T(8,128)(2,1)S(1)} %far.1), channel_id=1, source_target_pairs={{0,3},{1,2},{2,1},{3,0},{4,7},{5,6},{6,5},{7,4},{8,11},{9,10},{10,... | collective-permute-start | bytes 1572872 | tf_op jit(solution)/shard_map/ppermute | solution.py:344
  101.4 36.0 %collective-permute-start.16 = (bf16[2,2,2,32,128]{4,3,2,1,0:T(8,128)(2,1)S(1)}, bf16[2,2,2,32,128]{4,3,2,1,0:T(8,128)(2,1)S(1)}, u32[]{:S(2)}, u32[]{:S(2)}) collective-permute-start(bf16[2,2,2,32,128]{4,3,2,1,0:T(8,128)(2,1)S(1)} %get-tuple-element.18), channel_id=1, source_target_pairs={{0,29},{1,28},{2,31},{3,30},{4,25},{5,24},{6,27},{7,26},{8,21},{9,... | collective-permute-start | bytes 196616 | tf_op jit(solution)/shard_map/ppermute | solution.py:344
  130.5 7.0 %collective-permute-start.15 = (bf16[2,2,2,32,128]{4,3,2,1,0:T(8,128)(2,1)S(1)}, bf16[2,2,2,32,128]{4,3,2,1,0:T(8,128)(2,1)S(1)}, u32[]{:S(2)}, u32[]{:S(2)}) collective-permute-start(bf16[2,2,2,32,128]{4,3,2,1,0:T(8,128)(2,1)S(1)} %get-tuple-element.19), channel_id=1, source_target_pairs={{0,28},{1,29},{2,30},{3,31},{4,24},{5,25},{6,26},{7,27},{8,20},{9,... | collective-permute-start | bytes 196616 | tf_op jit(solution)/shard_map/ppermute | solution.py:344
  131.5 6.8 %collective-permute-start.14 = (bf16[2,2,2,32,128]{4,3,2,1,0:T(8,128)(2,1)S(1)}, bf16[2,2,2,32,128]{4,3,2,1,0:T(8,128)(2,1)S(1)}, u32[]{:S(2)}, u32[]{:S(2)}) collective-permute-start(bf16[2,2,2,32,128]{4,3,2,1,0:T(8,128)(2,1)S(1)} %get-tuple-element.20), channel_id=1, source_target_pairs={{0,25},{1,24},{2,27},{3,26},{4,29},{5,28},{6,31},{7,30},{8,17},{9,... | collective-permute-start | bytes 196616 | tf_op jit(solution)/shard_map/ppermute | solution.py:344
  132.2 6.7 %collective-permute-start.13 = (bf16[2,2,2,32,128]{4,3,2,1,0:T(8,128)(2,1)S(1)}, bf16[2,2,2,32,128]{4,3,2,1,0:T(8,128)(2,1)S(1)}, u32[]{:S(2)}, u32[]{:S(2)}) collective-permute-start(bf16[2,2,2,32,128]{4,3,2,1,0:T(8,128)(2,1)S(1)} %get-tuple-element.21), channel_id=1, source_target_pairs={{0,24},{1,25},{2,26},{3,27},{4,28},{5,29},{6,30},{7,31},{8,16},{9,... | collective-permute-start | bytes 196616 | tf_op jit(solution)/shard_map/ppermute | solution.py:344
  132.9 8.9 %collective-permute-start.12 = (bf16[2,2,2,32,128]{4,3,2,1,0:T(8,128)(2,1)S(1)}, bf16[2,2,2,32,128]{4,3,2,1,0:T(8,128)(2,1)S(1)}, u32[]{:S(2)}, u32[]{:S(2)}) collective-permute-start(bf16[2,2,2,32,128]{4,3,2,1,0:T(8,128)(2,1)S(1)} %get-tuple-element.22), channel_id=1, source_target_pairs={{0,21},{1,20},{2,23},{3,22},{4,17},{5,16},{6,19},{7,18},{8,29},{9,... | collective-permute-start | bytes 196616 | tf_op jit(solution)/shard_map/ppermute | solution.py:344
  137.4 5.5 %collective-permute-start.11 = (bf16[2,2,2,32,128]{4,3,2,1,0:T(8,128)(2,1)S(1)}, bf16[2,2,2,32,128]{4,3,2,1,0:T(8,128)(2,1)S(1)}, u32[]{:S(2)}, u32[]{:S(2)}) collective-permute-start(bf16[2,2,2,32,128]{4,3,2,1,0:T(8,128)(2,1)S(1)} %get-tuple-element.23), channel_id=1, source_target_pairs={{0,20},{1,21},{2,22},{3,23},{4,16},{5,17},{6,18},{7,19},{8,28},{9,... | collective-permute-start | bytes 196616 | tf_op jit(solution)/shard_map/ppermute | solution.py:344
  137.4 6.7 %collective-permute-start.10 = (bf16[2,2,2,32,128]{4,3,2,1,0:T(8,128)(2,1)S(1)}, bf16[2,2,2,32,128]{4,3,2,1,0:T(8,128)(2,1)S(1)}, u32[]{:S(2)}, u32[]{:S(2)}) collective-permute-start(bf16[2,2,2,32,128]{4,3,2,1,0:T(8,128)(2,1)S(1)} %get-tuple-element.24), channel_id=1, source_target_pairs={{0,17},{1,16},{2,19},{3,18},{4,21},{5,20},{6,23},{7,22},{8,25},{9,... | collective-permute-start | bytes 196616 | tf_op jit(solution)/shard_map/ppermute | solution.py:344
  138.3 6.6 %collective-permute-start.9 = (bf16[2,2,2,32,128]{4,3,2,1,0:T(8,128)(2,1)S(1)}, bf16[2,2,2,32,128]{4,3,2,1,0:T(8,128)(2,1)S(1)}, u32[]{:S(2)}, u32[]{:S(2)}) collective-permute-start(bf16[2,2,2,32,128]{4,3,2,1,0:T(8,128)(2,1)S(1)} %get-tuple-element.25), channel_id=1, source_target_pairs={{0,16},{1,17},{2,18},{3,19},{4,20},{5,21},{6,22},{7,23},{8,24},{9,... | collective-permute-start | bytes 196616 | tf_op jit(solution)/shard_map/ppermute | solution.py:344
  138.9 7.0 %collective-permute-start.8 = (bf16[2,2,2,32,128]{4,3,2,1,0:T(8,128)(2,1)S(1)}, bf16[2,2,2,32,128]{4,3,2,1,0:T(8,128)(2,1)S(1)}, u32[]{:S(2)}, u32[]{:S(2)}) collective-permute-start(bf16[2,2,2,32,128]{4,3,2,1,0:T(8,128)(2,1)S(1)} %get-tuple-element.26), channel_id=1, source_target_pairs={{0,13},{1,12},{2,15},{3,14},{4,9},{5,8},{6,11},{7,10},{8,5},{9,4},... | collective-permute-start | bytes 196616 | tf_op jit(solution)/shard_map/ppermute | solution.py:344
  141.8 4.7 %collective-permute-start.7 = (bf16[2,2,2,32,128]{4,3,2,1,0:T(8,128)(2,1)S(1)}, bf16[2,2,2,32,128]{4,3,2,1,0:T(8,128)(2,1)S(1)}, u32[]{:S(2)}, u32[]{:S(2)}) collective-permute-start(bf16[2,2,2,32,128]{4,3,2,1,0:T(8,128)(2,1)S(1)} %get-tuple-element.27), channel_id=1, source_target_pairs={{0,12},{1,13},{2,14},{3,15},{4,8},{5,9},{6,10},{7,11},{8,4},{9,5},... | collective-permute-start | bytes 196616 | tf_op jit(solution)/shard_map/ppermute | solution.py:344
  142.9 4.9 %collective-permute-start.6 = (bf16[2,2,2,32,128]{4,3,2,1,0:T(8,128)(2,1)S(1)}, bf16[2,2,2,32,128]{4,3,2,1,0:T(8,128)(2,1)S(1)}, u32[]{:S(2)}, u32[]{:S(2)}) collective-permute-start(bf16[2,2,2,32,128]{4,3,2,1,0:T(8,128)(2,1)S(1)} %get-tuple-element.28), channel_id=1, source_target_pairs={{0,9},{1,8},{2,11},{3,10},{4,13},{5,12},{6,15},{7,14},{8,1},{9,0},... | collective-permute-start | bytes 196616 | tf_op jit(solution)/shard_map/ppermute | solution.py:344
  144.1 5.2 %collective-permute-start.5 = (bf16[2,2,2,32,128]{4,3,2,1,0:T(8,128)(2,1)S(1)}, bf16[2,2,2,32,128]{4,3,2,1,0:T(8,128)(2,1)S(1)}, u32[]{:S(2)}, u32[]{:S(2)}) collective-permute-start(bf16[2,2,2,32,128]{4,3,2,1,0:T(8,128)(2,1)S(1)} %get-tuple-element.29), channel_id=1, source_target_pairs={{0,8},{1,9},{2,10},{3,11},{4,12},{5,13},{6,14},{7,15},{8,0},{9,1},... | collective-permute-start | bytes 196616 | tf_op jit(solution)/shard_map/ppermute | solution.py:344
  144.9 4.4 %collective-permute-start.4 = (bf16[2,2,2,32,128]{4,3,2,1,0:T(8,128)(2,1)S(1)}, bf16[2,2,2,32,128]{4,3,2,1,0:T(8,128)(2,1)S(1)}, u32[]{:S(2)}, u32[]{:S(2)}) collective-permute-start(bf16[2,2,2,32,128]{4,3,2,1,0:T(8,128)(2,1)S(1)} %get-tuple-element.30), channel_id=1, source_target_pairs={{0,5},{1,4},{2,7},{3,6},{4,1},{5,0},{6,3},{7,2},{8,13},{9,12},{10,... | collective-permute-start | bytes 196616 | tf_op jit(solution)/shard_map/ppermute | solution.py:344
  145.9 3.4 %collective-permute-start.3 = (bf16[2,2,2,32,128]{4,3,2,1,0:T(8,128)(2,1)S(1)}, bf16[2,2,2,32,128]{4,3,2,1,0:T(8,128)(2,1)S(1)}, u32[]{:S(2)}, u32[]{:S(2)}) collective-permute-start(bf16[2,2,2,32,128]{4,3,2,1,0:T(8,128)(2,1)S(1)} %get-tuple-element.31), channel_id=1, source_target_pairs={{0,4},{1,5},{2,6},{3,7},{4,0},{5,1},{6,2},{7,3},{8,12},{9,13},{10,... | collective-permute-start | bytes 196616 | tf_op jit(solution)/shard_map/ppermute | solution.py:344
  146.5 4.6 %collective-permute-start.2 = (bf16[2,2,2,32,128]{4,3,2,1,0:T(8,128)(2,1)S(1)}, bf16[2,2,2,32,128]{4,3,2,1,0:T(8,128)(2,1)S(1)}, u32[]{:S(2)}, u32[]{:S(2)}) collective-permute-start(bf16[2,2,2,32,128]{4,3,2,1,0:T(8,128)(2,1)S(1)} %get-tuple-element.32), channel_id=1, source_target_pairs={{0,1},{1,0},{2,3},{3,2},{4,5},{5,4},{6,7},{7,6},{8,9},{9,8},{10,11... | collective-permute-start | bytes 196616 | tf_op jit(solution)/shard_map/ppermute | solution.py:344

commit v5 on v4

--- a/solution.py
+++ b/solution.py
@@ -152,14 +152,19 @@
 def prepare_kernel(axes, begin, own, samples, taps, high, low, step, *refs):
     tail, rows, taps_out, step_out, phase, table, high_in, low_in, sems = refs
     frames = samples.shape[1]
-    last = pl.ds(begin - ROWS, frames - begin + ROWS)
+    held = frames - begin + ROWS
+    cut = held // 2 // ROWS * ROWS
+    spans = [(pol, start, size) for pol in range(samples.shape[0]) for start, size in ((0, cut), (cut, held - cut))]
     moves = [
         (high, high_in),
         (low, low_in),
         (step, step_out),
         (samples.at[:, pl.ds(frames - ROWS, ROWS)], tail),
-        (samples.at[:, last], rows),
         (taps, taps_out),
+        *(
+            (samples.at[pol, pl.ds(begin - ROWS + start, size)], rows.at[pol, pl.ds(start, size)])
+            for pol, start, size in spans
+        ),
     ]
     copies = [pltpu.make_async_copy(source, to, sems.at[i]) for i, (source, to) in enumerate(moves)]
     for copy in copies:
@@ -359,7 +364,7 @@
         ],
         in_specs=[hbm] * 5,
         out_specs=[vmem] * 6,
-        scratch_shapes=[pltpu.VMEM(high.shape, high.dtype), pltpu.VMEM(low.shape, low.dtype), dma((6,))],
+        scratch_shapes=[pltpu.VMEM(high.shape, high.dtype), pltpu.VMEM(low.shape, low.dtype), dma((5 + 2 * pols,))],
         compiler_params=pltpu.CompilerParams(vmem_limit_bytes=VMEM_LIMIT),
         name="prepare",
     )(*fixed)

time: 155 us -> 155 us (level)
  no operation moved by 1% of the time
where the time goes in v5:
time: 155 us; the launch traced here: 154 us
  waiting for transfers between devices  66.4 us (43%)
  starting transfers between devices  57.1 us (37%)
  Pallas kernels  23.8 us (15%)
  local copies, waits for them, and re-layouts  6.74 us (4%)
    ppermute x16, waiting for transfers between devices, swap(): return lax.ppermute(part, both, [(i, i ^ by) for i in range(devices)])  61.8 us
    ppermute x16, starting transfers between devices, swap(): return lax.ppermute(part, both, [(i, i ^ by) for i in range(devices)])  48.6 us
    pallas_call x2, Pallas kernels, compute(): pl.pallas_call(functools.partial(compute_kernel, axes, kind, at, own), ou...  16.6 us
    unnamed x12, local copies, waits for them, and re-layouts  6.64 us
    ppermute x1, waiting for transfers between devices, local(): halo = lax.ppermute(tail, both, [(i, i + 1) for i in range(devices - 1)])  4.66 us
    all_to_all x1, starting transfers between devices, local(): lax.all_to_all(part, both, split_axis=0, concat_axis=0, tiled=True)  4.56 us
    ppermute x1, starting transfers between devices, local(): halo = lax.ppermute(tail, both, [(i, i + 1) for i in range(devices - 1)])  4.01 us
  transfers between devices with their start and end apart: 18, of which 5 were waited for; matrix products, arithmetic and copies ran while one was open for 0% of the time, Pallas kernels for 5%

profile of v5, /device:TPU:1, one launch (start us, length us, event | category | flops | bytes accessed | tf_op | source)
XLA Modules:
  0.0 154.2 jit_solution(14612331192251077831)
XLA Ops:
  0.0 1.5 prepare.1
  1.5 1.0 copy-done
  2.5 1.0 copy-done.2
  3.4 1.0 copy-done.4
  4.4 4.0 %collective-permute-start = (bf16[2,8,2048]{2,1,0:T(8,128)(2,1)S(1)}, bf16[2,8,2048]{2,1,0:T(8,128)(2,1)S(1)}, u32[]{:S(2)}, u32[]{:S(2)}) collective-permute-start(bf16[2,8,2048]{2,1,0:T(8,128)(2,1)S(1)} %get-tuple-element.11), channel_id=1, source_target_pairs={{0,1},{1,2},{2,3},{3,4},{4,5},{5,6},{6,7},{7,8},{8,9},{9,10},{10,1... | collective-permute-start | bytes 196616 | tf_op jit(solution)/shard_map/ppermute | solution.py:371
  8.5 4.7 %collective-permute-done.refs_0_ = bf16[2,8,2048]{2,1,0:T(8,128)(2,1)S(1)} collective-permute-done((bf16[2,8,2048]{2,1,0:T(8,128)(2,1)S(1)}, bf16[2,8,2048]{2,1,0:T(8,128)(2,1)S(1)}, u32[]{:S(2)}, u32[]{:S(2)}) %collective-permute-start) | collective-permute-done | bytes 65568 | tf_op jit(solution)/shard_map/ppermute | solution.py:371
  13.1 12.5 %shard_map.55 = bf16[32,2,2,32,384]{4,3,2,1,0:T(8,128)(2,1)} custom-call(bf16[2,512,2048]{2,1,0:T(8,128)(2,1)} %samples.5, bf16[2,8,2048]{2,1,0:T(8,128)(2,1)S(1)} %collective-permute-done.refs_0_, f32[8,2048]{1,0:T(8,128)} %refs_1_.3, f32[2,64,128]{2,1,0:T(8,128)} %constant.6.clone.high.refs_2_, f32[2,16,128]{2,1,0:T(8,128)} %constant.7.clone.low.refs_3_, ...), custom_call_target="tpu_custom_call" | custom-call | flops 6442450944 | bytes 6291456 | tf_op jit(solution)/shard_map/pallas_call | solution.py:322
  25.6 4.6 %all-to-all-start = ((bf16[32,2,2,32,384]{4,3,2,1,0:T(8,128)(2,1)}), bf16[32,2,2,32,384]{4,3,2,1,0:T(8,128)(2,1)S(1)}, u32[]{:S(2)}, u32[]{:S(2)}) async-start(bf16[32,2,2,32,384]{4,3,2,1,0:T(8,128)(2,1)} %shard_map.55), calls=%async_computation | async-start | bytes 6291456 | tf_op jit(solution)/shard_map/all_to_all | solution.py:392
  30.2 1.2 copy-done.1
  31.4 1.2 copy-done.3
  32.6 1.2 copy-done.5
  33.9 2.6 %far.1 = bf16[16,2,2,32,128]{4,3,2,1,0:T(8,128)(2,1)S(1)} custom-call(bf16[2,136,2048]{2,1,0:T(8,128)(2,1)S(1)} %copy-done.1, f32[8,2048]{1,0:T(8,128)S(1)} %get-tuple-element.13.taps, f32[2,8,16,128]{3,2,1,0:T(8,128)S(1)} %get-tuple-element.14.step, f32[2,1024,128]{2,1,0:T(8,128)S(1)} %copy-done.3, bf16[2,256,1024]{2,1,0:T(8,128)(2,1)S(1)} %copy-done.5), custom_call_target="tpu_custom_call" | custom-call | flops 1073741824 | bytes 2097152 | tf_op jit(solution)/shard_map/far/pallas_call | solution.py:372
  36.5 3.3 %collective-permute-start.1 = (bf16[16,2,2,32,128]{4,3,2,1,0:T(8,128)(2,1)S(1)}, bf16[16,2,2,32,128]{4,3,2,1,0:T(8,128)(2,1)S(1)}, u32[]{:S(2)}, u32[]{:S(2)}) collective-permute-start(bf16[16,2,2,32,128]{4,3,2,1,0:T(8,128)(2,1)S(1)} %far.1), channel_id=1, source_target_pairs={{0,3},{1,2},{2,1},{3,0},{4,7},{5,6},{6,5},{7,4},{8,11},{9,10},{10,... | collective-permute-start | bytes 1572872 | tf_op jit(solution)/shard_map/ppermute | solution.py:349
  39.7 57.4 %collective-permute-done.1.refs_0_ = bf16[16,2,2,32,128]{4,3,2,1,0:T(8,128)(2,1)S(1)} collective-permute-done((bf16[16,2,2,32,128]{4,3,2,1,0:T(8,128)(2,1)S(1)}, bf16[16,2,2,32,128]{4,3,2,1,0:T(8,128)(2,1)S(1)}, u32[]{:S(2)}, u32[]{:S(2)}) %collective-permute-start.1) | collective-permute-done | bytes 524320 | tf_op jit(solution)/shard_map/ppermute | solution.py:349
  97.2 4.1 %shard_map.56 = bf16[16,2,2,2,32,128]{5,4,3,2,1,0:T(8,128)(2,1)S(1)} custom-call(bf16[2,512,2048]{2,1,0:T(8,128)(2,1)} %samples.5, bf16[16,2,2,32,128]{4,3,2,1,0:T(8,128)(2,1)S(1)} %collective-permute-done.1.refs_0_, f32[8,2048]{1,0:T(8,128)} %refs_1_.3, f32[2,64,128]{2,1,0:T(8,128)} %constant.6.clone.high.refs_2_, f32[2,16,128]{2,1,0:T(8,128)} %constant.7.clone.low.refs_3_, ...), custom_call_target="tpu_custom_call" | custom-call | flops 1073741824 | bytes 2097152 | tf_op jit(solution)/shard_map/pallas_call | solution.py:322
  101.4 29.1 %collective-permute-start.16 = (bf16[2,2,2,32,128]{4,3,2,1,0:T(8,128)(2,1)S(1)}, bf16[2,2,2,32,128]{4,3,2,1,0:T(8,128)(2,1)S(1)}, u32[]{:S(2)}, u32[]{:S(2)}) collective-permute-start(bf16[2,2,2,32,128]{4,3,2,1,0:T(8,128)(2,1)S(1)} %get-tuple-element.18), channel_id=1, source_target_pairs={{0,29},{1,28},{2,31},{3,30},{4,25},{5,24},{6,27},{7,26},{8,21},{9,... | collective-permute-start | bytes 196616 | tf_op jit(solution)/shard_map/ppermute | solution.py:349
  130.5 1.1 collective-permute-start.15
  131.5 0.7 collective-permute-start.14
  132.2 0.7 collective-permute-start.13
  132.9 4.5 %collective-permute-start.12 = (bf16[2,2,2,32,128]{4,3,2,1,0:T(8,128)(2,1)S(1)}, bf16[2,2,2,32,128]{4,3,2,1,0:T(8,128)(2,1)S(1)}, u32[]{:S(2)}, u32[]{:S(2)}) collective-permute-start(bf16[2,2,2,32,128]{4,3,2,1,0:T(8,128)(2,1)S(1)} %get-tuple-element.22), channel_id=1, source_target_pairs={{0,21},{1,20},{2,23},{3,22},{4,17},{5,16},{6,19},{7,18},{8,29},{9,... | collective-permute-start | bytes 196616 | tf_op jit(solution)/shard_map/ppermute | solution.py:349
  137.4 0.9 collective-permute-start.10
  138.3 0.6 collective-permute-start.9
  138.9 2.9 %collective-permute-start.8 = (bf16[2,2,2,32,128]{4,3,2,1,0:T(8,128)(2,1)S(1)}, bf16[2,2,2,32,128]{4,3,2,1,0:T(8,128)(2,1)S(1)}, u32[]{:S(2)}, u32[]{:S(2)}) collective-permute-start(bf16[2,2,2,32,128]{4,3,2,1,0:T(8,128)(2,1)S(1)} %get-tuple-element.26), channel_id=1, source_target_pairs={{0,13},{1,12},{2,15},{3,14},{4,9},{5,8},{6,11},{7,10},{8,5},{9,4},... | collective-permute-start | bytes 196616 | tf_op jit(solution)/shard_map/ppermute | solution.py:349
  141.8 1.1 collective-permute-done.11.refs_9_
  142.9 1.2 collective-permute-start.6
  144.1 0.7 collective-permute-start.5
  144.9 1.0 collective-permute-start.4
  146.5 1.4 collective-permute-start.2
  147.8 1.4 collective-permute-done.5.refs_3_
  149.3 1.8 %collective-permute-done.2.refs_0_ = bf16[2,2,2,32,128]{4,3,2,1,0:T(8,128)(2,1)S(1)} collective-permute-done((bf16[2,2,2,32,128]{4,3,2,1,0:T(8,128)(2,1)S(1)}, bf16[2,2,2,32,128]{4,3,2,1,0:T(8,128)(2,1)S(1)}, u32[]{:S(2)}, u32[]{:S(2)}) %collective-permute-start.2) | collective-permute-done | bytes 65568 | tf_op jit(solution)/shard_map/ppermute | solution.py:349
  151.1 1.2 place_near.1.held
  152.3 1.9 %place_main.1 = bf16[2,2,32,16384]{3,2,1,0:T(8,128)(2,1)} custom-call(bf16[32,2,2,32,384]{4,3,2,1,0:T(8,128)(2,1)S(1)} %all-to-all-done.block, bf16[2,2,32,16384]{3,2,1,0:T(8,128)(2,1)} %place_near.1.held), custom_call_target="tpu_custom_call", output_to_operand_aliasing={{}: (1, {})} | custom-call | tf_op jit(solution)/shard_map/place_main/pallas_call | solution.py:404
  (23 shorter events, 0.8 us)
Async XLA Ops:
  1.5 1.0 copy-start
  2.5 1.0 copy-start.2
  3.4 1.0 copy-start.4
  4.4 8.7 %collective-permute-start = (bf16[2,8,2048]{2,1,0:T(8,128)(2,1)S(1)}, bf16[2,8,2048]{2,1,0:T(8,128)(2,1)S(1)}, u32[]{:S(2)}, u32[]{:S(2)}) collective-permute-start(bf16[2,8,2048]{2,1,0:T(8,128)(2,1)S(1)} %get-tuple-element.11), channel_id=1, source_target_pairs={{0,1},{1,2},{2,3},{3,4},{4,5},{5,6},{6,7},{7,8},{8,9},{9,10},{10,1... | collective-permute-start | bytes 196616 | tf_op jit(solution)/shard_map/ppermute | solution.py:371
  25.6 126.7 %all-to-all-start = ((bf16[32,2,2,32,384]{4,3,2,1,0:T(8,128)(2,1)}), bf16[32,2,2,32,384]{4,3,2,1,0:T(8,128)(2,1)S(1)}, u32[]{:S(2)}, u32[]{:S(2)}) async-start(bf16[32,2,2,32,384]{4,3,2,1,0:T(8,128)(2,1)} %shard_map.55), calls=%async_computation | async-start | bytes 6291456 | tf_op jit(solution)/shard_map/all_to_all | solution.py:392
  30.2 1.3 copy-start.1
  31.4 1.2 copy-start.3
  32.6 1.2 copy-start.5
  36.5 60.7 %collective-permute-start.1 = (bf16[16,2,2,32,128]{4,3,2,1,0:T(8,128)(2,1)S(1)}, bf16[16,2,2,32,128]{4,3,2,1,0:T(8,128)(2,1)S(1)}, u32[]{:S(2)}, u32[]{:S(2)}) collective-permute-start(bf16[16,2,2,32,128]{4,3,2,1,0:T(8,128)(2,1)S(1)} %far.1), channel_id=1, source_target_pairs={{0,3},{1,2},{2,1},{3,0},{4,7},{5,6},{6,5},{7,4},{8,11},{9,10},{10,... | collective-permute-start | bytes 1572872 | tf_op jit(solution)/shard_map/ppermute | solution.py:349
  101.4 36.0 %collective-permute-start.16 = (bf16[2,2,2,32,128]{4,3,2,1,0:T(8,128)(2,1)S(1)}, bf16[2,2,2,32,128]{4,3,2,1,0:T(8,128)(2,1)S(1)}, u32[]{:S(2)}, u32[]{:S(2)}) collective-permute-start(bf16[2,2,2,32,128]{4,3,2,1,0:T(8,128)(2,1)S(1)} %get-tuple-element.18), channel_id=1, source_target_pairs={{0,29},{1,28},{2,31},{3,30},{4,25},{5,24},{6,27},{7,26},{8,21},{9,... | collective-permute-start | bytes 196616 | tf_op jit(solution)/shard_map/ppermute | solution.py:349
  130.5 7.0 %collective-permute-start.15 = (bf16[2,2,2,32,128]{4,3,2,1,0:T(8,128)(2,1)S(1)}, bf16[2,2,2,32,128]{4,3,2,1,0:T(8,128)(2,1)S(1)}, u32[]{:S(2)}, u32[]{:S(2)}) collective-permute-start(bf16[2,2,2,32,128]{4,3,2,1,0:T(8,128)(2,1)S(1)} %get-tuple-element.19), channel_id=1, source_target_pairs={{0,28},{1,29},{2,30},{3,31},{4,24},{5,25},{6,26},{7,27},{8,20},{9,... | collective-permute-start | bytes 196616 | tf_op jit(solution)/shard_map/ppermute | solution.py:349
  131.5 6.8 %collective-permute-start.14 = (bf16[2,2,2,32,128]{4,3,2,1,0:T(8,128)(2,1)S(1)}, bf16[2,2,2,32,128]{4,3,2,1,0:T(8,128)(2,1)S(1)}, u32[]{:S(2)}, u32[]{:S(2)}) collective-permute-start(bf16[2,2,2,32,128]{4,3,2,1,0:T(8,128)(2,1)S(1)} %get-tuple-element.20), channel_id=1, source_target_pairs={{0,25},{1,24},{2,27},{3,26},{4,29},{5,28},{6,31},{7,30},{8,17},{9,... | collective-permute-start | bytes 196616 | tf_op jit(solution)/shard_map/ppermute | solution.py:349
  132.2 6.7 %collective-permute-start.13 = (bf16[2,2,2,32,128]{4,3,2,1,0:T(8,128)(2,1)S(1)}, bf16[2,2,2,32,128]{4,3,2,1,0:T(8,128)(2,1)S(1)}, u32[]{:S(2)}, u32[]{:S(2)}) collective-permute-start(bf16[2,2,2,32,128]{4,3,2,1,0:T(8,128)(2,1)S(1)} %get-tuple-element.21), channel_id=1, source_target_pairs={{0,24},{1,25},{2,26},{3,27},{4,28},{5,29},{6,30},{7,31},{8,16},{9,... | collective-permute-start | bytes 196616 | tf_op jit(solution)/shard_map/ppermute | solution.py:349
  132.9 8.9 %collective-permute-start.12 = (bf16[2,2,2,32,128]{4,3,2,1,0:T(8,128)(2,1)S(1)}, bf16[2,2,2,32,128]{4,3,2,1,0:T(8,128)(2,1)S(1)}, u32[]{:S(2)}, u32[]{:S(2)}) collective-permute-start(bf16[2,2,2,32,128]{4,3,2,1,0:T(8,128)(2,1)S(1)} %get-tuple-element.22), channel_id=1, source_target_pairs={{0,21},{1,20},{2,23},{3,22},{4,17},{5,16},{6,19},{7,18},{8,29},{9,... | collective-permute-start | bytes 196616 | tf_op jit(solution)/shard_map/ppermute | solution.py:349
  137.4 5.5 %collective-permute-start.11 = (bf16[2,2,2,32,128]{4,3,2,1,0:T(8,128)(2,1)S(1)}, bf16[2,2,2,32,128]{4,3,2,1,0:T(8,128)(2,1)S(1)}, u32[]{:S(2)}, u32[]{:S(2)}) collective-permute-start(bf16[2,2,2,32,128]{4,3,2,1,0:T(8,128)(2,1)S(1)} %get-tuple-element.23), channel_id=1, source_target_pairs={{0,20},{1,21},{2,22},{3,23},{4,16},{5,17},{6,18},{7,19},{8,28},{9,... | collective-permute-start | bytes 196616 | tf_op jit(solution)/shard_map/ppermute | solution.py:349
  137.4 6.7 %collective-permute-start.10 = (bf16[2,2,2,32,128]{4,3,2,1,0:T(8,128)(2,1)S(1)}, bf16[2,2,2,32,128]{4,3,2,1,0:T(8,128)(2,1)S(1)}, u32[]{:S(2)}, u32[]{:S(2)}) collective-permute-start(bf16[2,2,2,32,128]{4,3,2,1,0:T(8,128)(2,1)S(1)} %get-tuple-element.24), channel_id=1, source_target_pairs={{0,17},{1,16},{2,19},{3,18},{4,21},{5,20},{6,23},{7,22},{8,25},{9,... | collective-permute-start | bytes 196616 | tf_op jit(solution)/shard_map/ppermute | solution.py:349
  138.3 6.6 %collective-permute-start.9 = (bf16[2,2,2,32,128]{4,3,2,1,0:T(8,128)(2,1)S(1)}, bf16[2,2,2,32,128]{4,3,2,1,0:T(8,128)(2,1)S(1)}, u32[]{:S(2)}, u32[]{:S(2)}) collective-permute-start(bf16[2,2,2,32,128]{4,3,2,1,0:T(8,128)(2,1)S(1)} %get-tuple-element.25), channel_id=1, source_target_pairs={{0,16},{1,17},{2,18},{3,19},{4,20},{5,21},{6,22},{7,23},{8,24},{9,... | collective-permute-start | bytes 196616 | tf_op jit(solution)/shard_map/ppermute | solution.py:349
  138.9 7.0 %collective-permute-start.8 = (bf16[2,2,2,32,128]{4,3,2,1,0:T(8,128)(2,1)S(1)}, bf16[2,2,2,32,128]{4,3,2,1,0:T(8,128)(2,1)S(1)}, u32[]{:S(2)}, u32[]{:S(2)}) collective-permute-start(bf16[2,2,2,32,128]{4,3,2,1,0:T(8,128)(2,1)S(1)} %get-tuple-element.26), channel_id=1, source_target_pairs={{0,13},{1,12},{2,15},{3,14},{4,9},{5,8},{6,11},{7,10},{8,5},{9,4},... | collective-permute-start | bytes 196616 | tf_op jit(solution)/shard_map/ppermute | solution.py:349
  141.8 4.7 %collective-permute-start.7 = (bf16[2,2,2,32,128]{4,3,2,1,0:T(8,128)(2,1)S(1)}, bf16[2,2,2,32,128]{4,3,2,1,0:T(8,128)(2,1)S(1)}, u32[]{:S(2)}, u32[]{:S(2)}) collective-permute-start(bf16[2,2,2,32,128]{4,3,2,1,0:T(8,128)(2,1)S(1)} %get-tuple-element.27), channel_id=1, source_target_pairs={{0,12},{1,13},{2,14},{3,15},{4,8},{5,9},{6,10},{7,11},{8,4},{9,5},... | collective-permute-start | bytes 196616 | tf_op jit(solution)/shard_map/ppermute | solution.py:349
  142.9 4.9 %collective-permute-start.6 = (bf16[2,2,2,32,128]{4,3,2,1,0:T(8,128)(2,1)S(1)}, bf16[2,2,2,32,128]{4,3,2,1,0:T(8,128)(2,1)S(1)}, u32[]{:S(2)}, u32[]{:S(2)}) collective-permute-start(bf16[2,2,2,32,128]{4,3,2,1,0:T(8,128)(2,1)S(1)} %get-tuple-element.28), channel_id=1, source_target_pairs={{0,9},{1,8},{2,11},{3,10},{4,13},{5,12},{6,15},{7,14},{8,1},{9,0},... | collective-permute-start | bytes 196616 | tf_op jit(solution)/shard_map/ppermute | solution.py:349
  144.1 5.2 %collective-permute-start.5 = (bf16[2,2,2,32,128]{4,3,2,1,0:T(8,128)(2,1)S(1)}, bf16[2,2,2,32,128]{4,3,2,1,0:T(8,128)(2,1)S(1)}, u32[]{:S(2)}, u32[]{:S(2)}) collective-permute-start(bf16[2,2,2,32,128]{4,3,2,1,0:T(8,128)(2,1)S(1)} %get-tuple-element.29), channel_id=1, source_target_pairs={{0,8},{1,9},{2,10},{3,11},{4,12},{5,13},{6,14},{7,15},{8,0},{9,1},... | collective-permute-start | bytes 196616 | tf_op jit(solution)/shard_map/ppermute | solution.py:349
  144.9 4.4 %collective-permute-start.4 = (bf16[2,2,2,32,128]{4,3,2,1,0:T(8,128)(2,1)S(1)}, bf16[2,2,2,32,128]{4,3,2,1,0:T(8,128)(2,1)S(1)}, u32[]{:S(2)}, u32[]{:S(2)}) collective-permute-start(bf16[2,2,2,32,128]{4,3,2,1,0:T(8,128)(2,1)S(1)} %get-tuple-element.30), channel_id=1, source_target_pairs={{0,5},{1,4},{2,7},{3,6},{4,1},{5,0},{6,3},{7,2},{8,13},{9,12},{10,... | collective-permute-start | bytes 196616 | tf_op jit(solution)/shard_map/ppermute | solution.py:349
  145.9 3.4 %collective-permute-start.3 = (bf16[2,2,2,32,128]{4,3,2,1,0:T(8,128)(2,1)S(1)}, bf16[2,2,2,32,128]{4,3,2,1,0:T(8,128)(2,1)S(1)}, u32[]{:S(2)}, u32[]{:S(2)}) collective-permute-start(bf16[2,2,2,32,128]{4,3,2,1,0:T(8,128)(2,1)S(1)} %get-tuple-element.31), channel_id=1, source_target_pairs={{0,4},{1,5},{2,6},{3,7},{4,0},{5,1},{6,2},{7,3},{8,12},{9,13},{10,... | collective-permute-start | bytes 196616 | tf_op jit(solution)/shard_map/ppermute | solution.py:349
  146.5 4.6 %collective-permute-start.2 = (bf16[2,2,2,32,128]{4,3,2,1,0:T(8,128)(2,1)S(1)}, bf16[2,2,2,32,128]{4,3,2,1,0:T(8,128)(2,1)S(1)}, u32[]{:S(2)}, u32[]{:S(2)}) collective-permute-start(bf16[2,2,2,32,128]{4,3,2,1,0:T(8,128)(2,1)S(1)} %get-tuple-element.32), channel_id=1, source_target_pairs={{0,1},{1,0},{2,3},{3,2},{4,5},{5,4},{6,7},{7,6},{8,9},{9,8},{10,11... | collective-permute-start | bytes 196616 | tf_op jit(solution)/shard_map/ppermute | solution.py:349
